TPU v7x, 16 devices: a 4x2x1 block of a 4x4x8 slice. The times are simulated.
16 devices in a mesh: dp: 2 (over y, z), kv: 8 (over x, core).
Axes of the slice: x: 4, y: 2, z: 1, core: 2. Of those that a mesh axis runs over, the one named last changes fastest.
The devices are a block of a 4x4x8 slice.
Arguments:
- x_first: bfloat16 [32, 1536], P('dp'), parts along dimension 0
- next_emb: bfloat16 [2, 32, 1536], P(None, 'dp'), parts along dimension 1
- k_cache: bfloat16 [32, 4096, 8, 64], P('dp', 'kv'), parts along dimension 0
- v_cache: bfloat16 [32, 4096, 8, 64], P('dp', 'kv'), parts along dimension 0
- seq_len: int32 [32], P('dp'), parts along dimension 0
- ln1_gain: float32 [1536], replicated
- ln1_bias: float32 [1536], replicated
- w_q: bfloat16 [1536, 1536], replicated
- b_q: float32 [1536], replicated
- w_k: bfloat16 [1536, 512], replicated
- b_k: float32 [512], replicated
- w_v: bfloat16 [1536, 512], replicated
- b_v: float32 [512], replicated
- w_o: bfloat16 [1536, 1536], replicated
- b_o: float32 [1536], replicated
- ln2_gain: float32 [1536], replicated
- ln2_bias: float32 [1536], replicated
- w_router: bfloat16 [1536, 40], replicated
- w_gate: bfloat16 [40, 1536, 512], P(None, None, 'kv')
- w_up: bfloat16 [40, 1536, 512], P(None, None, 'kv')
- w_down: bfloat16 [40, 512, 1536], P(None, 'kv')
- long_factor: float32 [32], replicated
- expert_idx: int32 [3, 32, 8], P(None, 'dp'), parts along dimension 1
- route_mask: int32 [3, 32, 8, 40], P(None, 'dp'), parts along dimension 1
Outputs:
- output 1: bfloat16 [3, 32, 1536], P(None, 'dp'), parts along dimension 1
- output 2: bfloat16 [32, 3, 8, 64], P('dp'), parts along dimension 0
- output 3: bfloat16 [32, 3, 8, 64], P('dp'), parts along dimension 0
There are 2 independent parts. A program takes and returns all parts, laid end to end along the dimension named above; an argument that names none is the same for every part.
All inputs are finite; a program needn't handle non-finite values.
Results may differ from a plain program's by a relative error of at most 0.0119208.
Values sent between devices are 32-bit elements.
A program may use at most 768 MiB of HBM per device.

v0:
```python
import functools
import math

import jax
import jax.numpy as jnp
from jax import lax
from jax.experimental import pallas as pl
from jax.experimental.pallas import tpu as pltpu
from jax.sharding import PartitionSpec as P

ROPE_BASE = 10000.0
ROPE_MSCALE = math.sqrt(1.0 + math.log(32.0) / math.log(4096.0))
NORM_EPS = 1e-5
NEG_FILL = -1e30
LANES = 128
SUBL = 8
F32 = jnp.float32
BF16 = jnp.bfloat16
NT = (((1,), (1,)), ((), ()))


def norm_rows(x, gain, bias):
    mean = jnp.mean(x, axis=-1, keepdims=True)
    cent = x - mean
    var = jnp.mean(cent * cent, axis=-1, keepdims=True)
    return (cent * lax.rsqrt(var + NORM_EPS) * gain + bias).astype(BF16)


def layer_kernel(dims, x_first, next_emb, k_hbm, v_hbm, len_hbm, g1_hbm, b1_hbm, wq_hbm, bq_hbm, wk_hbm, bk_hbm, wv_hbm, bv_hbm, wo_hbm, bo_hbm, g2_hbm, b2_hbm, wr_hbm, wg_hbm, wu_hbm, wd_hbm, lf_hbm, idx_hbm, mask_hbm,
                 hid_out, tk_out, tv_out,
                 x_s, len_s, lf_s, vec_s, bk_s, bv_s, wr_s, idx_s, mask_s,
                 wq_s, wk_s, wv_s, wo_s, k_s, v_s, wg_s, wu_s, wd_s,
                 q_s, kt_s, vt_s, hs_s, p_s, msg_s, recv_s, obuf_s, xm_s, gex_s, u_s, pbuf_s, rbuf_s, ybuf_s,
                 small_sem, wq_sem, wkv_sem, wo_sem, k_sem, v_sem, exp_sem, wd_sem,
                 a_send, a_recv, o_send, o_recv, p_send, p_recv, y_send, y_recv):
    n, steps, batch, heads_kv, hd, group, shard, n_exp, ff, dm = dims
    rows = steps * batch
    gs_n = group * steps
    qrows = (gs_n + 1) * heads_kv
    hdk = heads_kv * hd
    n_hp = hdk // LANES
    half_b = batch // 2
    me = lax.axis_index('kv')
    chip = me // 2
    core = lax.rem(me, 2)

    barrier = pltpu.get_barrier_semaphore()
    for d in range(1, n):
        pl.semaphore_signal(barrier, inc=1, device_id={'kv': lax.rem(me + d, n)}, device_id_type=pl.DeviceIdType.MESH)

    smalls = [(x_first, x_s.at[0])] + [(next_emb.at[i], x_s.at[i + 1]) for i in range(steps - 1)]
    smalls += [(len_hbm, len_s), (lf_hbm, lf_s)]
    smalls += [(src, vec_s.at[i]) for i, src in enumerate((g1_hbm, b1_hbm, bq_hbm, bo_hbm, g2_hbm, b2_hbm))]
    smalls += [(bk_hbm, bk_s), (bv_hbm, bv_s), (wr_hbm, wr_s), (idx_hbm, idx_s), (mask_hbm, mask_s)]
    small_copies = [pltpu.make_async_copy(src, dst, small_sem.at[i]) for i, (src, dst) in enumerate(smalls)]
    qw = wq_s.shape[2]
    wq_copies = [pltpu.make_async_copy(wq_hbm.at[:, pl.ds(i * qw, qw)], wq_s.at[i], wq_sem.at[i]) for i in range(n_hp)]
    wkv_copies = [pltpu.make_async_copy(wk_hbm, wk_s, wkv_sem.at[0]), pltpu.make_async_copy(wv_hbm, wv_s, wkv_sem.at[1])]
    for cp in small_copies + wq_copies + wkv_copies:
        cp.start()

    def seq_of(it):
        return lax.rem(core * half_b + it, batch)

    def k_copy(b):
        return pltpu.make_async_copy(k_hbm.at[b], k_s.at[b], k_sem.at[b])

    def v_copy(b):
        return pltpu.make_async_copy(v_hbm.at[b], v_s.at[b], v_sem.at[b])

    for it in range(batch):
        k_copy(seq_of(it)).start()
    for it in range(batch):
        v_copy(seq_of(it)).start()
    wo_copies = [pltpu.make_async_copy(wo_hbm.at[:, g], wo_s.at[g], wo_sem.at[g]) for g in range(group)]
    n_ec = wg_s.shape[0] // LANES
    ec_part = 4
    ec_rows = wg_s.shape[0] // ec_part
    exp_copies = []
    for i in range(ec_part):
        sl = pl.ds(i * ec_rows, ec_rows)
        exp_copies.append(pltpu.make_async_copy(wg_hbm.at[sl], wg_s.at[sl], exp_sem.at[0, i]))
        exp_copies.append(pltpu.make_async_copy(wu_hbm.at[sl], wu_s.at[sl], exp_sem.at[1, i]))
    wd_copies = [pltpu.make_async_copy(wd_hbm.at[pl.ds(i * ec_rows, ec_rows)], wd_s.at[pl.ds(i * ec_rows, ec_rows)], wd_sem.at[i]) for i in range(ec_part)]

    for cp in small_copies:
        cp.wait()

    g1, b1, bq, bo, g2, b2 = [vec_s[i].reshape(1, dm) for i in range(6)]
    x = x_s[...].reshape(rows, dm).astype(F32)
    h = norm_rows(x, g1, b1)

    lane1 = lax.broadcasted_iota(jnp.int32, (1, LANES), 1)
    half_dim = hd // 2
    jlane = lax.rem(lane1, half_dim)
    lfv = jnp.zeros((1, LANES), F32)
    for j in range(half_dim):
        lfv = jnp.where(jlane == j, lf_s[j], lfv)
    inv = 1.0 / (lfv * jnp.exp(jlane.astype(F32) * (2.0 * math.log(ROPE_BASE) / hd)))
    subb = lax.broadcasted_iota(jnp.int32, (batch, LANES), 0)
    pos = jnp.zeros((batch, LANES), jnp.int32)
    for b in range(batch):
        pos = jnp.where(subb == b, len_s[b], pos)
    ang = jnp.concatenate([(pos + s).astype(F32) * inv for s in range(steps)], axis=0)
    cos = jnp.cos(ang) * ROPE_MSCALE
    sin = jnp.sin(ang) * ROPE_MSCALE
    lane_r = lax.broadcasted_iota(jnp.int32, (rows, LANES), 1)
    sin = jnp.where(lax.rem(lane_r, hd) < half_dim, -sin, sin)
    low_half = lax.rem(lane_r, hd) < half_dim
    low_head = lane_r < hd

    def rope(t):
        t = t.astype(BF16).astype(F32)
        rot = jnp.where(low_half, pltpu.roll(t, LANES - half_dim, 1), pltpu.roll(t, half_dim, 1))
        return (t * cos + rot * sin).astype(BF16).astype(F32)

    for hp in range(n_hp):
        wq_copies[hp].wait()
        t = jnp.dot(h, wq_s[hp], preferred_element_type=F32) + bq[:, hp * qw:(hp + 1) * qw]
        parts = [rope(t[:, c * LANES:(c + 1) * LANES]) for c in range(qw // LANES)]
        for g in range(group):
            first, second = g, group + g
            a, a_hi = parts[first // 2], first % 2
            c, c_hi = parts[second // 2], second % 2
            a = pltpu.roll(a, hd, 1) if a_hi else a
            c = c if c_hi else pltpu.roll(c, hd, 1)
            q_s[hp, g * steps:(g + 1) * steps] = jnp.where(low_head, a, c).reshape(steps, batch, LANES)
    for cp in wkv_copies:
        cp.wait()
    t = jnp.dot(h, wk_s[...], preferred_element_type=F32) + bk_s[...].reshape(1, hdk)
    for hp in range(n_hp):
        kt_s[hp] = rope(t[:, hp * LANES:(hp + 1) * LANES]).reshape(steps, batch, LANES)
    t = (jnp.dot(h, wv_s[...], preferred_element_type=F32) + bv_s[...].reshape(1, hdk)).astype(BF16).astype(F32)
    for hp in range(n_hp):
        vt_s[hp] = t[:, hp * LANES:(hp + 1) * LANES].reshape(steps, batch, LANES)

    for cp in wo_copies + exp_copies + wd_copies:
        cp.start()

    tpos = me * shard + lax.broadcasted_iota(jnp.int32, (1, shard), 1)
    diag = lax.broadcasted_iota(jnp.int32, (heads_kv, hdk), 0) == lax.broadcasted_iota(jnp.int32, (heads_kv, hdk), 1) // hd
    ident = lax.broadcasted_iota(jnp.int32, (qrows, LANES), 0) == lax.broadcasted_iota(jnp.int32, (qrows, LANES), 1)

    def to_row(col):
        return jnp.sum(jnp.where(ident, col, 0.0), axis=0, keepdims=True)

    def scores(it, _):
        b = seq_of(it)
        k_copy(b).wait()
        blocks = []
        for gs in range(gs_n):
            qrow = jnp.concatenate([q_s[hp, gs, pl.ds(b, 1), :] for hp in range(n_hp)], axis=1)
            blocks.append(jnp.where(diag, qrow, 0.0))
        blocks.append(jnp.zeros((heads_kv, hdk), F32))
        qbd = jnp.concatenate(blocks, axis=0).astype(BF16)
        keep = tpos < len_s[b]
        sc = jnp.dot(qbd, k_s[b], preferred_element_type=F32) * (hd ** -0.5)
        sc = jnp.where(keep, sc, NEG_FILL)
        m = jnp.max(sc, axis=1, keepdims=True)
        w = jnp.where(keep, jnp.exp(sc - m), 0.0)
        p_s[b] = w.astype(BF16)
        half, b8 = b // half_b, lax.rem(b, half_b)
        msg_s[half, 0, gs_n, pl.ds(b8, 1), :] = to_row(m)
        msg_s[half, 0, gs_n + 1, pl.ds(b8, 1), :] = to_row(jnp.sum(w, axis=1, keepdims=True))
        return 0

    def outputs(it, _):
        b = seq_of(it)
        v_copy(b).wait()
        o = lax.dot_general(p_s[b], v_s[b], NT, preferred_element_type=F32)
        half, b8 = b // half_b, lax.rem(b, half_b)
        for gs in range(gs_n):
            row = jnp.sum(jnp.where(diag, o[gs * heads_kv:(gs + 1) * heads_kv], 0.0), axis=0, keepdims=True)
            for hp in range(n_hp):
                msg_s[half, hp, gs, pl.ds(b8, 1), :] = row[:, hp * LANES:(hp + 1) * LANES]
        return 0

    def a_copy(half, hp, slot):
        return pltpu.make_async_remote_copy(
            src_ref=msg_s.at[half, hp], dst_ref=recv_s.at[me], send_sem=a_send.at[slot], recv_sem=a_recv.at[me],
            device_id={'kv': hp * 2 + half}, device_id_type=pl.DeviceIdType.MESH)

    sends = []
    for turn in range(2):
        lax.fori_loop(turn * half_b, (turn + 1) * half_b, scores, 0, unroll=4)
        lax.fori_loop(turn * half_b, (turn + 1) * half_b, outputs, 0, unroll=4)
        half = lax.rem(core + turn, 2)
        mt, lt = msg_s[half, 0, gs_n], msg_s[half, 0, gs_n + 1]
        for hp in range(1, n_hp):
            msg_s[half, hp, gs_n] = pltpu.roll(mt, LANES - 2 * hp, 1)
            msg_s[half, hp, gs_n + 1] = pltpu.roll(lt, LANES - 2 * hp, 1)
        if turn == 0:
            pl.semaphore_wait(barrier, n - 1)
        for dx in (2, 1, 3, 0):
            hp = lax.rem(chip + dx, n_hp)
            if turn == 0 and dx == 0:
                recv_s[me] = msg_s[half, hp]
            else:
                cp = a_copy(half, hp, len(sends))
                cp.start()
                sends.append(cp)

    lane8 = lax.broadcasted_iota(jnp.int32, (half_b, LANES), 1)
    low8 = lane8 < hd
    brow = pl.ds(pl.multiple_of(core * half_b, half_b), half_b)
    m_tail = jnp.full((half_b, LANES), NEG_FILL, F32)
    l_tail = jnp.zeros((half_b, LANES), F32)
    for gs in range(gs_n):
        s = gs % steps
        qt = q_s[chip, gs, brow, :]
        cols = []
        for slot in range(s + 1):
            prod = qt * kt_s[chip, slot, brow, :]
            lo = jnp.sum(jnp.where(low8, prod, 0.0), axis=1, keepdims=True)
            hi = jnp.sum(jnp.where(low8, 0.0, prod), axis=1, keepdims=True)
            cols.append(jnp.where(low8, lo, hi) * (hd ** -0.5))
        mx = functools.reduce(jnp.maximum, cols)
        ws = [jnp.exp(c - mx) for c in cols]
        lsum = functools.reduce(jnp.add, ws)
        acc = functools.reduce(jnp.add, [w.astype(BF16).astype(F32) * vt_s[chip, slot, brow, :] for slot, w in enumerate(ws)])
        recv_s[n, gs] = acc
        for j in range(2):
            sel = lane8 == gs * heads_kv + j
            m_tail = jnp.where(sel, mx[:, j * hd:j * hd + 1], m_tail)
            l_tail = jnp.where(sel, lsum[:, j * hd:j * hd + 1], l_tail)


    def a_wait(src):
        pltpu.make_async_remote_copy(
            src_ref=msg_s.at[0, 0], dst_ref=recv_s.at[src], send_sem=a_send.at[0], recv_sem=a_recv.at[src],
            device_id={'kv': me}, device_id_type=pl.DeviceIdType.MESH).wait_recv()

    for d in range(1, n):
        a_wait(lax.rem(me + d, n))
    ms = [recv_s[src, gs_n] for src in range(n)] + [m_tail]
    ls = [recv_s[src, gs_n + 1] for src in range(n)] + [l_tail]
    mx = functools.reduce(jnp.maximum, ms)
    al = [jnp.exp(m - mx) for m in ms]
    tot = functools.reduce(jnp.add, [a * l for a, l in zip(al, ls)])
    for gs in range(gs_n):
        def spread(t):
            lane = gs * heads_kv
            return jnp.where(low8, t[:, lane:lane + 1], t[:, lane + 1:lane + 2])
        acc = functools.reduce(jnp.add, [spread(a) * recv_s[src, gs] for src, a in enumerate(al)])
        obuf_s[me, gs] = (acc / spread(tot)).astype(BF16).astype(F32)

    def bcast(buf, send, recv):
        out = []
        for i, d in enumerate((4, 5, 2, 6, 3, 7, 1)):
            cp = pltpu.make_async_remote_copy(
                src_ref=buf.at[me], dst_ref=buf.at[me], send_sem=send.at[i], recv_sem=recv.at[me],
                device_id={'kv': lax.rem(me + d, n)}, device_id_type=pl.DeviceIdType.MESH)
            cp.start()
            out.append(cp)
        return out

    def wait_all(buf, send, recv):
        for d in range(1, n):
            src = lax.rem(me + d, n)
            pltpu.make_async_remote_copy(
                src_ref=buf.at[src], dst_ref=buf.at[src], send_sem=send.at[0], recv_sem=recv.at[src],
                device_id={'kv': me}, device_id_type=pl.DeviceIdType.MESH).wait_recv()

    sends += bcast(obuf_s, o_send, o_recv)

    for src_s, dst in ((kt_s, tk_out), (vt_s, tv_out)):
        for hp in range(n_hp):
            t = src_s[hp].reshape(rows, LANES)
            hs_s[:, 2 * hp, :] = t[:, :hd]
            hs_s[:, 2 * hp + 1, :] = pltpu.roll(t, hd, 1)[:, :hd]
        for s in range(steps):
            dst[:, s] = hs_s[s * batch:(s + 1) * batch].astype(BF16)

    for cp in wo_copies:
        cp.wait()
    wait_all(obuf_s, o_send, o_recv)
    pieces = []
    for g in range(group):
        for hp in range(n_hp):
            pieces.append(jnp.concatenate([obuf_s[hp * 2 + half, g * steps + s] for s in range(steps) for half in range(2)], axis=0))
    o_all = jnp.concatenate(pieces, axis=1).astype(BF16)
    x = x_s[...].reshape(rows, dm).astype(F32)
    xm = (x + jnp.dot(o_all, wo_s[...].reshape(dm, dm), preferred_element_type=F32) + bo).astype(BF16).astype(F32)
    xm_s[...] = xm.reshape(2, rows // 2, dm)
    h2 = norm_rows(xm, g2, b2)

    logits = lax.dot_general(h2, wr_s[...], NT, preferred_element_type=F32)
    topk = mask_s.shape[1]
    e_iota = lax.broadcasted_iota(jnp.int32, (topk, n_exp), 1)
    grows = []
    for s in range(steps):
        ids = idx_s[s]
        for b in range(batch):
            r = s * batch + b
            lg = jnp.where(mask_s[r] == 1, logits[r:r + 1, :], NEG_FILL)
            ex = jnp.exp(lg - jnp.max(lg, axis=1, keepdims=True))
            pr = ex / jnp.sum(ex, axis=1, keepdims=True)
            grows.append(jnp.sum(jnp.where(ids[:, b:b + 1] == e_iota, pr, 0.0), axis=0, keepdims=True))
    gates = jnp.concatenate(grows, axis=0)
    per = LANES // ff
    for c in range(n_ec):
        gex_s[c] = jnp.where(low_head, gates[:, per * c:per * c + 1], gates[:, per * c + 1:per * c + 2])

    for cp in exp_copies:
        cp.wait()

    def expert(c, _):
        rs = pl.ds(pl.multiple_of(c * LANES, LANES), LANES)
        ag = lax.dot_general(h2, wg_s[rs, :], NT, preferred_element_type=F32)
        au = lax.dot_general(h2, wu_s[rs, :], NT, preferred_element_type=F32)
        u_s[c] = (gex_s[c] * (ag * (1.0 / (1.0 + jnp.exp(-ag)))) * au).astype(BF16)
        return 0

    lax.fori_loop(0, n_ec, expert, 0, unroll=2)

    for cp in wd_copies:
        cp.wait()
    cw = dm // n_hp
    hr = rows // 2
    u = jnp.concatenate([u_s[c] for c in range(n_ec)], axis=1)
    k = 0
    for dx in (2, 1, 3, 0):
        cq = lax.rem(chip + dx, n_hp)
        part = jnp.dot(u, wd_s[:, pl.ds(pl.multiple_of(cq * cw, LANES), cw)], preferred_element_type=F32)
        part = part.astype(BF16).astype(F32)
        for half in range(2):
            pbuf_s[cq * 2 + half] = part[half * hr:(half + 1) * hr]
        for dc in range(2):
            half = lax.rem(core + 1 + dc, 2)
            owner = cq * 2 + half
            if dx == 0 and dc == 1:
                rbuf_s[me] = pbuf_s[me]
            else:
                cp = pltpu.make_async_remote_copy(
                    src_ref=pbuf_s.at[owner], dst_ref=rbuf_s.at[me], send_sem=p_send.at[k], recv_sem=p_recv.at[me],
                    device_id={'kv': owner}, device_id_type=pl.DeviceIdType.MESH)
                cp.start()
                sends.append(cp)
                k += 1
    wait_all(rbuf_s, p_send, p_recv)
    tot = functools.reduce(jnp.add, [rbuf_s[src] for src in range(n)])
    y = xm_s[core, :, pl.ds(pl.multiple_of(chip * cw, LANES), cw)] + tot
    ybuf_s[me] = y.astype(BF16).astype(F32)
    sends += bcast(ybuf_s, y_send, y_recv)
    wait_all(ybuf_s, y_send, y_recv)
    for cq in range(n_hp):
        blk = jnp.concatenate([ybuf_s[cq * 2], ybuf_s[cq * 2 + 1]], axis=0)
        hid_out[:, :, cq * cw:(cq + 1) * cw] = blk.astype(BF16).reshape(steps, batch, cw)
    for cp in sends:
        cp.wait_send()


def solution(mesh):
    n = mesh.shape['kv']

    def layer_steps(x_first, next_emb, k_cache, v_cache, seq_len, ln1_gain, ln1_bias, w_q, b_q, w_k, b_k, w_v, b_v, w_o, b_o, ln2_gain, ln2_bias, w_router, w_gate, w_up, w_down, long_factor, expert_idx, route_mask):
        batch, shard, heads_kv, hd = k_cache.shape
        dm = x_first.shape[1]
        q_heads = w_q.shape[1] // hd
        group = q_heads // heads_kv
        steps = next_emb.shape[0] + 1
        n_exp, _, ff = w_gate.shape
        topk = expert_idx.shape[-1]
        rows = steps * batch
        hdk = heads_kv * hd
        n_hp = hdk // LANES
        gs_n = group * steps
        qrows = (gs_n + 1) * heads_kv
        fe = n_exp * ff
        dims = (n, steps, batch, heads_kv, hd, group, shard, n_exp, ff, dm)
        args = (
            x_first, next_emb,
            jnp.transpose(k_cache, (0, 2, 3, 1)).reshape(batch, hdk, shard),
            jnp.transpose(v_cache, (0, 2, 3, 1)).reshape(batch, hdk, shard),
            seq_len, ln1_gain, ln1_bias, w_q, b_q, w_k, b_k, w_v, b_v,
            w_o.reshape(heads_kv, group, hd, dm), b_o, ln2_gain, ln2_bias,
            jnp.transpose(w_router),
            jnp.transpose(w_gate, (0, 2, 1)).reshape(fe, dm),
            jnp.transpose(w_up, (0, 2, 1)).reshape(fe, dm),
            w_down.reshape(fe, dm), long_factor,
            jnp.transpose(expert_idx, (0, 2, 1)),
            route_mask.reshape(rows, topk, n_exp),
        )
        any_spec = pl.BlockSpec(memory_space=pl.ANY)
        vmem_spec = pl.BlockSpec(memory_space=pltpu.VMEM)
        dma = pltpu.SemaphoreType.DMA
        vm = pltpu.VMEM
        scratch = [
            vm((steps, batch, dm), BF16), pltpu.SMEM((batch,), jnp.int32), pltpu.SMEM((hd // 2,), F32),
            vm((6, dm), F32), vm((hdk,), F32), vm((hdk,), F32), vm((n_exp, dm), BF16),
            vm((steps, topk, batch), jnp.int32), vm((rows, topk, n_exp), jnp.int32),
            vm((n_hp, dm, dm // n_hp), BF16), vm((dm, hdk), BF16), vm((dm, hdk), BF16),
            vm((group, heads_kv, hd, dm), BF16), vm((batch, hdk, shard), BF16), vm((batch, hdk, shard), BF16),
            vm((fe, dm), BF16), vm((fe, dm), BF16), vm((fe, dm), BF16),
            vm((n_hp, gs_n, batch, LANES), F32), vm((n_hp, steps, batch, LANES), F32), vm((n_hp, steps, batch, LANES), F32),
            vm((rows, heads_kv, hd), F32), vm((batch, qrows, shard), BF16),
            vm((2, n_hp, gs_n + 2, SUBL, LANES), F32), vm((n + 1, gs_n + 2, SUBL, LANES), F32),
            vm((n, gs_n, SUBL, LANES), F32), vm((2, rows // 2, dm), F32),
            vm((fe // LANES, rows, LANES), F32), vm((fe // LANES, rows, LANES), BF16),
            vm((n, rows // 2, dm // n_hp), F32), vm((n, rows // 2, dm // n_hp), F32), vm((n, rows // 2, dm // n_hp), F32),
            dma((steps + 13,)), dma((n_hp,)), dma((2,)), dma((group,)), dma((batch,)), dma((batch,)), dma((2, 4)), dma((4,)),
            dma((n,)), dma((n,)), dma((n,)), dma((n,)), dma((n,)), dma((n,)), dma((n,)), dma((n,)),
        ]
        return pl.pallas_call(
            functools.partial(layer_kernel, dims),
            out_shape=(
                jax.ShapeDtypeStruct((steps, batch, dm), BF16),
                jax.ShapeDtypeStruct((batch, steps, heads_kv, hd), BF16),
                jax.ShapeDtypeStruct((batch, steps, heads_kv, hd), BF16),
            ),
            in_specs=[any_spec] * len(args),
            out_specs=(vmem_spec,) * 3,
            scratch_shapes=scratch,
            compiler_params=pltpu.CompilerParams(collective_id=0, has_side_effects=True, vmem_limit_bytes=66 * 1024 * 1024 - 2 * 1024 * 1024),
        )(*args)

    replicated = P()
    in_specs = (P('dp'), P(None, 'dp'), P('dp', 'kv'), P('dp', 'kv'), P('dp')) + (replicated,) * 13 + (P(None, None, 'kv'), P(None, None, 'kv'), P(None, 'kv'), replicated, P(None, 'dp'), P(None, 'dp'))
    out_specs = (P(None, 'dp'), P('dp'), P('dp'))
    return jax.shard_map(layer_steps, mesh=mesh, in_specs=in_specs, out_specs=out_specs, check_vma=False)
```

profile of v0, /device:TPU:113, one launch (start us, length us, event | category | flops | bytes accessed | tf_op | source)
XLA Modules:
  0.0 61.0 jit_solution(14727686511236433037)
XLA Ops:
  0.6 55.7 %shard_map.247 = (bf16[3,16,1536]{2,1,0:T(8,128)(2,1)}, bf16[16,3,8,64]{3,2,1,0:T(8,128)(2,1)}, bf16[16,3,8,64]{3,2,1,0:T(8,128)(2,1)}) custom-call(bf16[16,1536]{1,0:T(8,128)(2,1)} %x_first.1, bf16[2,16,1536]{2,1,0:T(8,128)(2,1)} %next_emb.1, bf16[16,512,512]{2,1,0:T(8,128)(2,1)} %bitcast.17, bf16[16,512,512]{2,1,0:T(8,128)(2,1)} %bitcast.18, s32[16]{0:T(128)} %len_hbm.1, ...), custom_call_target="tpu_custom_call" | custom-call | tf_op jit(solution)/shard_map/pallas_call | solution.py:404
  56.3 1.6 %copy.30 = bf16[3,16,1536]{2,1,0:T(8,128)(2,1)} copy(bf16[3,16,1536]{2,1,0:T(8,128)(2,1)} %get-tuple-element.6) | data formatting | bytes 294912
  57.9 1.5 %copy.31 = bf16[16,3,8,64]{3,2,1,0:T(8,128)(2,1)} copy(bf16[16,3,8,64]{3,2,1,0:T(8,128)(2,1)} %get-tuple-element.7) | data formatting | bytes 98304
  59.4 1.5 %copy.32 = bf16[16,3,8,64]{3,2,1,0:T(8,128)(2,1)} copy(bf16[16,3,8,64]{3,2,1,0:T(8,128)(2,1)} %get-tuple-element.8) | data formatting | bytes 98304
where the time goes:
time: 61.2 us; the launch traced here: 61 us
  Pallas kernels  55.7 us (91%)
  local copies, waits for them, and re-layouts  4.67 us (8%)
  between operations  0.65 us (1%)
    pallas_call x1, Pallas kernels, layer_steps(): pl.pallas_call(functools.partial(layer_kernel, dims), out_shape=(jax.Shap...  55.7 us
    unnamed x3, local copies, waits for them, and re-layouts  4.67 us

commit v1 on v0

v1 whole, which is shorter than its diff:
```python
import functools
import math

import jax
import jax.numpy as jnp
from jax import lax
from jax.experimental import pallas as pl
from jax.experimental.pallas import tpu as pltpu
from jax.sharding import PartitionSpec as P

ROPE_BASE = 10000.0
ROPE_MSCALE = math.sqrt(1.0 + math.log(32.0) / math.log(4096.0))
NORM_EPS = 1e-5
NEG_FILL = -1e30
LANES = 128
SUBL = 8
F32 = jnp.float32
BF16 = jnp.bfloat16
NT = (((1,), (1,)), ((), ()))


def norm_rows(x, gain, bias):
    mean = jnp.mean(x, axis=-1, keepdims=True)
    cent = x - mean
    var = jnp.mean(cent * cent, axis=-1, keepdims=True)
    return (cent * lax.rsqrt(var + NORM_EPS) * gain + bias).astype(BF16)


def layer_kernel(dims, x_first, next_emb, k_hbm, v_hbm, len_hbm, g1_hbm, b1_hbm, wq_hbm, bq_hbm, wk_hbm, bk_hbm, wv_hbm, bv_hbm, wo_hbm, bo_hbm, g2_hbm, b2_hbm, wr_hbm, wg_hbm, wu_hbm, wd_hbm, lf_hbm, idx_hbm, mask_hbm,
                 hid_out, tk_out, tv_out,
                 x_s, len_s, lf_s, vec_s, bk_s, bv_s, wr_s, idx_s, mask_s,
                 wq_s, wk_s, wv_s, wo_s, k_s, v_s, wg_s, wu_s, wd_s,
                 q_s, kt_s, vt_s, hs_s, p_s, msg_s, pair_s, amsg_s, recv_s, obuf_s, xm_s, gex_s, u_s, pbuf_s, ppair_s, psum_s, rbuf_s, ybuf_s,
                 hid_s, tk_s, tv_s,
                 small_sem, wq_sem, wkv_sem, wo_sem, k_sem, v_sem, exp_sem, wd_sem, out_sem,
                 pair_sem, a_send, a_recv, o_send, o_recv, d_send, d_recv, p_send, p_recv, y_send, y_recv):
    n, steps, batch, heads_kv, hd, group, shard, n_exp, ff, dm = dims
    rows = steps * batch
    gs_n = group * steps
    qrows = (gs_n + 1) * heads_kv
    hdk = heads_kv * hd
    n_hp = hdk // LANES
    half_b = batch // 2
    me = lax.axis_index('kv')
    chip = me // 2
    core = lax.rem(me, 2)
    other = 1 - core
    partner = chip * 2 + other
    mesh_id = pl.DeviceIdType.MESH

    def remote(src, dst, send, recv, dev):
        return pltpu.make_async_remote_copy(src_ref=src, dst_ref=dst, send_sem=send, recv_sem=recv, device_id={'kv': dev}, device_id_type=mesh_id)

    vecs = (g1_hbm, b1_hbm, bq_hbm, bo_hbm, g2_hbm, b2_hbm)
    smalls = [(x_first, x_s.at[0], 0), (next_emb, x_s.at[pl.ds(1, steps - 1)], 0)]
    smalls += [(len_hbm, len_s, 1), (lf_hbm, lf_s, 2), (bk_hbm, bk_s, 3), (bv_hbm, bv_s, 4), (wr_hbm, wr_s, 5), (idx_hbm, idx_s, 6), (mask_hbm, mask_s, 7)]
    smalls += [(src, vec_s.at[i], 8 + i) for i, src in enumerate(vecs)]
    small_copies = [pltpu.make_async_copy(src, dst, small_sem.at[i]) for src, dst, i in smalls]
    small_waits = [pltpu.make_async_copy(x_s, x_s, small_sem.at[0])] + small_copies[2:]
    qw = wq_s.shape[2]
    wq_copies = [pltpu.make_async_copy(wq_hbm.at[:, pl.ds(i * qw, qw)], wq_s.at[i], wq_sem.at[i]) for i in range(n_hp)]
    wkv_copies = [pltpu.make_async_copy(wk_hbm, wk_s, wkv_sem.at[0]), pltpu.make_async_copy(wv_hbm, wv_s, wkv_sem.at[1])]
    for cp in small_copies + wq_copies + wkv_copies:
        cp.start()

    barrier = pltpu.get_barrier_semaphore()
    for d in range(1, n):
        pl.semaphore_signal(barrier, inc=1, device_id={'kv': lax.rem(me + d, n)}, device_id_type=mesh_id)

    quad = half_b // 2
    n_quad = batch // quad

    def quad_base(i):
        return pl.multiple_of((other if i < n_quad // 2 else core) * half_b + (i % 2) * quad, quad)

    def cache_copy(src, dst, sem, i):
        sl = pl.ds(quad_base(i), quad)
        return pltpu.make_async_copy(src.at[sl], dst.at[sl], sem.at[i])

    k_copies = [cache_copy(k_hbm, k_s, k_sem, i) for i in range(n_quad)]
    v_copies = [cache_copy(v_hbm, v_s, v_sem, i) for i in range(n_quad)]
    n_ec = wg_s.shape[0] // LANES

    def weight_start(src, dst, sem, parts=4):
        ec = src.shape[0] // parts
        for i in range(parts):
            pltpu.make_async_copy(src.at[pl.ds(i * ec, ec)], dst.at[pl.ds(i * ec, ec)], sem).start()

    def weight_wait(dst, sem):
        pltpu.make_async_copy(dst, dst, sem).wait()

    for cp in small_waits:
        cp.wait()

    g1, b1, bq, bo, g2, b2 = [vec_s[i].reshape(1, dm) for i in range(6)]
    x = x_s[...].reshape(rows, dm).astype(F32)
    h = norm_rows(x, g1, b1)

    lane1 = lax.broadcasted_iota(jnp.int32, (1, LANES), 1)
    half_dim = hd // 2
    jlane = lax.rem(lane1, half_dim)
    lfv = jnp.zeros((1, LANES), F32)
    for j in range(half_dim):
        lfv = jnp.where(jlane == j, lf_s[j], lfv)
    inv = 1.0 / (lfv * jnp.exp(jlane.astype(F32) * (2.0 * math.log(ROPE_BASE) / hd)))
    subb = lax.broadcasted_iota(jnp.int32, (batch, LANES), 0)
    pos = jnp.zeros((batch, LANES), jnp.int32)
    for b in range(batch):
        pos = jnp.where(subb == b, len_s[b], pos)
    ang = jnp.concatenate([(pos + s).astype(F32) * inv for s in range(steps)], axis=0)
    cos = jnp.cos(ang) * ROPE_MSCALE
    sin = jnp.sin(ang) * ROPE_MSCALE
    lane_r = lax.broadcasted_iota(jnp.int32, (rows, LANES), 1)
    sin = jnp.where(lax.rem(lane_r, hd) < half_dim, -sin, sin)
    low_half = lax.rem(lane_r, hd) < half_dim
    low_head = lane_r < hd

    def rope(t):
        t = t.astype(BF16).astype(F32)
        rot = jnp.where(low_half, pltpu.roll(t, LANES - half_dim, 1), pltpu.roll(t, half_dim, 1))
        return (t * cos + rot * sin).astype(BF16).astype(F32)

    def q_block(hp):
        t = jnp.dot(h, wq_s[hp], preferred_element_type=F32) + bq[:, hp * qw:(hp + 1) * qw]
        parts = [rope(t[:, c * LANES:(c + 1) * LANES]) for c in range(qw // LANES)]
        for g in range(group):
            first, second = g, group + g
            a, a_hi = parts[first // 2], first % 2
            c, c_hi = parts[second // 2], second % 2
            a = pltpu.roll(a, hd, 1) if a_hi else a
            c = c if c_hi else pltpu.roll(c, hd, 1)
            q_s[hp, g * steps:(g + 1) * steps] = jnp.where(low_head, a, c).reshape(steps, batch, LANES)

    wq_copies[0].wait()
    for cp in (k_copies[0], k_copies[1], v_copies[0], k_copies[2]):
        cp.start()
    wq_copies[1].wait()
    for hp in range(2):
        q_block(hp)
    for cp in wq_copies[2:] + wkv_copies:
        cp.wait()
    for cp in (v_copies[1], k_copies[3], v_copies[2], v_copies[3]):
        cp.start()
    for hp in range(2, n_hp):
        q_block(hp)
    t = jnp.dot(h, wk_s[...], preferred_element_type=F32) + bk_s[...].reshape(1, hdk)
    for hp in range(n_hp):
        kt_s[hp] = rope(t[:, hp * LANES:(hp + 1) * LANES]).reshape(steps, batch, LANES)
    t = (jnp.dot(h, wv_s[...], preferred_element_type=F32) + bv_s[...].reshape(1, hdk)).astype(BF16).astype(F32)
    for hp in range(n_hp):
        vt_s[hp] = t[:, hp * LANES:(hp + 1) * LANES].reshape(steps, batch, LANES)

    tpos = me * shard + lax.broadcasted_iota(jnp.int32, (1, shard), 1)
    diag = lax.broadcasted_iota(jnp.int32, (heads_kv, hdk), 0) == lax.broadcasted_iota(jnp.int32, (heads_kv, hdk), 1) // hd
    ident = lax.broadcasted_iota(jnp.int32, (qrows, LANES), 0) == lax.broadcasted_iota(jnp.int32, (qrows, LANES), 1)
    m_slot = n_hp * gs_n

    def to_row(col):
        return jnp.sum(jnp.where(ident, col, 0.0), axis=0, keepdims=True)

    def scores(i):
        base = quad_base(i)
        half = other if i < n_quad // 2 else core
        for j in range(quad):
            b = base + j
            blocks = []
            for gs in range(gs_n):
                qrow = jnp.concatenate([q_s[hp, gs, pl.ds(b, 1), :] for hp in range(n_hp)], axis=1)
                blocks.append(jnp.where(diag, qrow, 0.0))
            blocks.append(jnp.zeros((heads_kv, hdk), F32))
            qbd = jnp.concatenate(blocks, axis=0).astype(BF16)
            keep = tpos < len_s[b]
            sc = jnp.dot(qbd, k_s[b], preferred_element_type=F32) * (hd ** -0.5)
            sc = jnp.where(keep, sc, NEG_FILL)
            m = jnp.max(sc, axis=1, keepdims=True)
            w = jnp.where(keep, jnp.exp(sc - m), 0.0)
            p_s[b] = w.astype(BF16)
            b8 = (i % 2) * quad + j
            msg_s[half, m_slot, b8:b8 + 1, :] = to_row(m)
            msg_s[half, m_slot + 1, b8:b8 + 1, :] = to_row(jnp.sum(w, axis=1, keepdims=True))

    def outputs(i):
        base = quad_base(i)
        half = other if i < n_quad // 2 else core
        for j in range(quad):
            b = base + j
            o = lax.dot_general(p_s[b], v_s[b], NT, preferred_element_type=F32)
            b8 = (i % 2) * quad + j
            for gs in range(gs_n):
                row = jnp.sum(jnp.where(diag, o[gs * heads_kv:(gs + 1) * heads_kv], 0.0), axis=0, keepdims=True)
                for hp in range(n_hp):
                    msg_s[half, hp * gs_n + gs, b8:b8 + 1, :] = row[:, hp * LANES:(hp + 1) * LANES]

    sends = []
    pair_cp = remote(msg_s.at[other], pair_s, pair_sem.at[0], pair_sem.at[1], partner)
    for i in range(n_quad + 1):
        if i < n_quad:
            k_copies[i].wait()
        if i:
            v_copies[i - 1].wait()
        if i < n_quad:
            scores(i)
        if i:
            outputs(i - 1)
        if i == n_quad // 2:
            pl.semaphore_wait(barrier, n - 1)
            pair_cp.start()
            for g in range(group):
                pltpu.make_async_copy(wo_hbm.at[:, :, g], wo_s.at[:, g], wo_sem.at[0]).start()
            weight_start(wg_hbm, wg_s, exp_sem.at[0])
            weight_start(wu_hbm, wu_s, exp_sem.at[1])
            weight_start(wd_hbm, wd_s, wd_sem.at[0])
    pair_cp.wait_recv()

    lane8 = lax.broadcasted_iota(jnp.int32, (half_b, LANES), 1)
    low8 = lane8 < hd

    def spread(t, gs):
        lane = gs * heads_kv
        return jnp.where(low8, t[:, lane:lane + 1], t[:, lane + 1:lane + 2])

    ma, mb = msg_s[core, m_slot], pair_s[m_slot]
    mm = jnp.maximum(ma, mb)
    ea, eb = jnp.exp(ma - mm), jnp.exp(mb - mm)
    ll = ea * msg_s[core, m_slot + 1] + eb * pair_s[m_slot + 1]
    far = (2, 1, 3, 0)
    for dx in far:
        hp = lax.rem(chip + dx, n_hp)
        shift = lax.rem(LANES - 2 * hp, LANES)
        ra, rb = pltpu.roll(ea, shift, 1), pltpu.roll(eb, shift, 1)
        dst = recv_s.at[chip] if dx == 0 else amsg_s.at[dx]
        for gs in range(gs_n):
            dst[gs] = spread(ra, gs) * msg_s[core, hp * gs_n + gs] + spread(rb, gs) * pair_s[hp * gs_n + gs]
        dst[gs_n] = pltpu.roll(mm, shift, 1)
        dst[gs_n + 1] = pltpu.roll(ll, shift, 1)
    for k, dx in enumerate(far[:-1]):
        cp = remote(amsg_s.at[dx], recv_s.at[chip], a_send.at[k], a_recv.at[chip], lax.rem(chip + dx, n_hp) * 2 + core)
        cp.start()
        sends.append(cp)

    pair_cp.wait_send()
    brow = pl.ds(pl.multiple_of(core * half_b, half_b), half_b)
    m_tail = jnp.full((half_b, LANES), NEG_FILL, F32)
    l_tail = jnp.zeros((half_b, LANES), F32)
    for gs in range(gs_n):
        s = gs % steps
        qt = q_s[chip, gs, brow, :]
        cols = []
        for slot in range(s + 1):
            prod = qt * kt_s[chip, slot, brow, :]
            lo = jnp.sum(jnp.where(low8, prod, 0.0), axis=1, keepdims=True)
            hi = jnp.sum(jnp.where(low8, 0.0, prod), axis=1, keepdims=True)
            cols.append(jnp.where(low8, lo, hi) * (hd ** -0.5))
        mx = functools.reduce(jnp.maximum, cols)
        ws = [jnp.exp(c - mx) for c in cols]
        lsum = functools.reduce(jnp.add, ws)
        acc = functools.reduce(jnp.add, [w.astype(BF16).astype(F32) * vt_s[chip, slot, brow, :] for slot, w in enumerate(ws)])
        recv_s[n_hp, gs] = acc
        for j in range(2):
            sel = lane8 == gs * heads_kv + j
            m_tail = jnp.where(sel, mx[:, j * hd:j * hd + 1], m_tail)
            l_tail = jnp.where(sel, lsum[:, j * hd:j * hd + 1], l_tail)
    recv_s[n_hp, gs_n] = m_tail
    recv_s[n_hp, gs_n + 1] = l_tail

    for src_s, dst, out, i in ((kt_s, tk_s, tk_out, 0), (vt_s, tv_s, tv_out, 1)):
        for hp in range(n_hp):
            t = src_s[hp].reshape(rows, LANES)
            hs_s[:, 2 * hp, :] = t[:, :hd]
            hs_s[:, 2 * hp + 1, :] = pltpu.roll(t, hd, 1)[:, :hd]
        for s in range(steps):
            dst[:, s] = hs_s[s * batch:(s + 1) * batch].astype(BF16)
        pltpu.make_async_copy(dst, out, out_sem.at[i]).start()

    for dx in (1, 3, 2):
        src = lax.rem(chip + dx, n_hp)
        remote(recv_s.at[src], recv_s.at[src], a_send.at[0], a_recv.at[src], me).wait_recv()
    srcs = range(n_hp + 1)
    ms = [recv_s[src, gs_n] for src in srcs]
    mx = functools.reduce(jnp.maximum, ms)
    al = [jnp.exp(m - mx) for m in ms]
    tot = functools.reduce(jnp.add, [a * recv_s[src, gs_n + 1] for src, a in zip(srcs, al)])
    for gs in range(gs_n):
        acc = functools.reduce(jnp.add, [spread(a, gs) * recv_s[src, gs] for src, a in zip(srcs, al)])
        obuf_s[me, gs] = (acc / spread(tot, gs)).astype(BF16).astype(F32)

    order = (1, 3, 2)

    def gather_start(buf, send, recv):
        for i, dx in enumerate((2, 1, 3, 0)):
            dev = partner if dx == 0 else lax.rem(chip + dx, n_hp) * 2 + core
            cp = remote(buf.at[me], buf.at[me], send.at[i], recv.at[me], dev)
            cp.start()
            sends.append(cp)

    def arrived(buf, send, recv, src):
        remote(buf.at[src], buf.at[src], send.at[0], recv.at[src], me).wait_recv()

    def relay(buf, send, recv, i, dx):
        src = lax.rem(chip + dx, n_hp) * 2 + core
        arrived(buf, send, recv, src)
        cp = remote(buf.at[src], buf.at[src], send.at[n_hp + i], recv.at[src], partner)
        cp.start()
        sends.append(cp)

    gather_start(obuf_s, o_send, o_recv)
    weight_wait(wo_s, wo_sem.at[0])
    weight_wait(wg_s, exp_sem.at[0])
    weight_wait(wu_s, exp_sem.at[1])
    weight_wait(wd_s, wd_sem.at[0])

    def wo_part(cx):
        pieces = []
        for g in range(group):
            pieces.append(jnp.concatenate([obuf_s[cx * 2 + half, g * steps + s] for s in range(steps) for half in range(2)], axis=0))
        lhs = jnp.concatenate(pieces, axis=1).astype(BF16)
        return jnp.dot(lhs, wo_s[cx].reshape(group * LANES, dm), preferred_element_type=F32)

    arrived(obuf_s, o_send, o_recv, partner)
    acc = wo_part(chip)
    for i, dx in enumerate(order):
        relay(obuf_s, o_send, o_recv, i, dx)
        if i:
            cx = lax.rem(chip + order[i - 1], n_hp)
            arrived(obuf_s, o_send, o_recv, cx * 2 + other)
            acc = acc + wo_part(cx)
    cx = lax.rem(chip + order[-1], n_hp)
    arrived(obuf_s, o_send, o_recv, cx * 2 + other)
    acc = acc + wo_part(cx)
    x = x_s[...].reshape(rows, dm).astype(F32)
    xm = (x + acc + bo).astype(BF16).astype(F32)
    xm_s[...] = xm.reshape(2, rows // 2, dm)
    h2 = norm_rows(xm, g2, b2)

    logits = lax.dot_general(h2, wr_s[...], NT, preferred_element_type=F32)
    topk = mask_s.shape[1]
    e_iota = lax.broadcasted_iota(jnp.int32, (topk, n_exp), 1)
    grows = []
    for s in range(steps):
        ids = idx_s[s]
        for b in range(batch):
            r = s * batch + b
            lg = jnp.where(mask_s[r] == 1, logits[r:r + 1, :], NEG_FILL)
            ex = jnp.exp(lg - jnp.max(lg, axis=1, keepdims=True))
            pr = ex / jnp.sum(ex, axis=1, keepdims=True)
            grows.append(jnp.sum(jnp.where(ids[:, b:b + 1] == e_iota, pr, 0.0), axis=0, keepdims=True))
    gates = jnp.concatenate(grows, axis=0)
    per = LANES // ff

    def act(c):
        rs = pl.ds(c * LANES, LANES)
        ag = lax.dot_general(h2, wg_s[rs, :], NT, preferred_element_type=F32)
        au = lax.dot_general(h2, wu_s[rs, :], NT, preferred_element_type=F32)
        return ag * (1.0 / (1.0 + jnp.exp(-ag))), au

    peel = n_ec // 4
    for c in range(n_ec):
        gex_s[c] = jnp.where(low_head, gates[:, per * c:per * c + 1], gates[:, per * c + 1:per * c + 2])
    for c in range(peel):
        sg, au = act(c)
        u_s[c] = (gex_s[c] * sg * au).astype(BF16)

    def expert(i, _):
        for j in range(peel):
            c = i * peel + j
            sg, au = act(c)
            u_s[c] = (gex_s[c] * sg * au).astype(BF16)
        return 0

    lax.fori_loop(1, n_ec // peel, expert, 0)
    cw = dm // n_hp
    hr = rows // 2
    u = jnp.concatenate([u_s[c] for c in range(n_ec)], axis=1)

    def add_pair(k, cq, own):
        remote(ppair_s.at[cq], ppair_s.at[cq], d_send.at[0], d_recv.at[cq], me).wait_recv()
        tot = pbuf_s[cq, core] + ppair_s[cq]
        if own:
            return tot
        psum_s[cq] = tot
        cp = remote(psum_s.at[cq], rbuf_s.at[chip], p_send.at[k], p_recv.at[chip], cq * 2 + core)
        cp.start()
        sends.append(cp)

    down = (2, 1, 3, 0)
    for k, dx in enumerate(down):
        cq = lax.rem(chip + dx, n_hp)
        cols = pl.ds(pl.multiple_of(cq * cw, LANES), cw)
        part = jnp.dot(u, wd_s[:, cols], preferred_element_type=F32)
        pbuf_s[cq] = part.astype(BF16).astype(F32).reshape(2, hr, cw)
        cp = remote(pbuf_s.at[cq, other], ppair_s.at[cq], d_send.at[k], d_recv.at[cq], partner)
        cp.start()
        sends.append(cp)
        if k:
            add_pair(k - 1, lax.rem(chip + down[k - 1], n_hp), False)
    y = xm_s[core, :, pl.ds(pl.multiple_of(chip * cw, LANES), cw)] + add_pair(0, chip, True)
    for dx in (1, 3, 2):
        src = lax.rem(chip + dx, n_hp)
        remote(rbuf_s.at[src], rbuf_s.at[src], p_send.at[0], p_recv.at[src], me).wait_recv()
        y = y + rbuf_s[src]
    ybuf_s[me] = y.astype(BF16).astype(F32)
    gather_start(ybuf_s, y_send, y_recv)
    for i, dx in enumerate(order):
        relay(ybuf_s, y_send, y_recv, i, dx)
    for dx in (0,) + order:
        arrived(ybuf_s, y_send, y_recv, lax.rem(chip + dx, n_hp) * 2 + other)
    for cq in range(n_hp):
        blk = jnp.concatenate([ybuf_s[cq * 2], ybuf_s[cq * 2 + 1]], axis=0)
        hid_s[:, :, cq * cw:(cq + 1) * cw] = blk.astype(BF16).reshape(steps, batch, cw)
    hid_cp = pltpu.make_async_copy(hid_s, hid_out, out_sem.at[2])
    hid_cp.start()
    for cp in sends:
        cp.wait_send()
    pltpu.make_async_copy(tk_s, tk_out, out_sem.at[0]).wait()
    pltpu.make_async_copy(tv_s, tv_out, out_sem.at[1]).wait()
    hid_cp.wait()


def emit_kernel(*refs):
    k = len(refs) // 3
    ins, outs, bufs, sem = refs[:k], refs[k:2 * k], refs[2 * k:3 * k], refs[3 * k]
    loads = [pltpu.make_async_copy(ins[i], bufs[i], sem.at[0, i]) for i in range(k)]
    stores = [pltpu.make_async_copy(bufs[i], outs[i], sem.at[1, i]) for i in range(k)]
    for cp in loads:
        cp.start()
    for ld, st in zip(loads, stores):
        ld.wait()
        st.start()
    for cp in stores:
        cp.wait()


def solution(mesh):
    n = mesh.shape['kv']

    def layer_steps(x_first, next_emb, k_cache, v_cache, seq_len, ln1_gain, ln1_bias, w_q, b_q, w_k, b_k, w_v, b_v, w_o, b_o, ln2_gain, ln2_bias, w_router, w_gate, w_up, w_down, long_factor, expert_idx, route_mask):
        batch, shard, heads_kv, hd = k_cache.shape
        dm = x_first.shape[1]
        q_heads = w_q.shape[1] // hd
        group = q_heads // heads_kv
        steps = next_emb.shape[0] + 1
        n_exp, _, ff = w_gate.shape
        topk = expert_idx.shape[-1]
        rows = steps * batch
        hdk = heads_kv * hd
        n_hp = hdk // LANES
        gs_n = group * steps
        qrows = (gs_n + 1) * heads_kv
        fe = n_exp * ff
        dims = (n, steps, batch, heads_kv, hd, group, shard, n_exp, ff, dm)
        args = (
            x_first, next_emb,
            jnp.transpose(k_cache, (0, 2, 3, 1)).reshape(batch, hdk, shard),
            jnp.transpose(v_cache, (0, 2, 3, 1)).reshape(batch, hdk, shard),
            seq_len, ln1_gain, ln1_bias, w_q, b_q, w_k, b_k, w_v, b_v,
            w_o.reshape(n_hp, 2, group, hd, dm), b_o, ln2_gain, ln2_bias,
            jnp.transpose(w_router),
            jnp.transpose(w_gate, (0, 2, 1)).reshape(fe, dm),
            jnp.transpose(w_up, (0, 2, 1)).reshape(fe, dm),
            w_down.reshape(fe, dm), long_factor,
            jnp.transpose(expert_idx, (0, 2, 1)),
            route_mask.reshape(rows, topk, n_exp),
        )
        any_spec = pl.BlockSpec(memory_space=pl.ANY)
        dma = pltpu.SemaphoreType.DMA
        vm = pltpu.VMEM
        outs = (
            jax.ShapeDtypeStruct((steps, batch, dm), BF16),
            jax.ShapeDtypeStruct((batch, steps, heads_kv, hd), BF16),
            jax.ShapeDtypeStruct((batch, steps, heads_kv, hd), BF16),
        )
        blk = vm((n, rows // 2, dm // n_hp), F32)
        qblk = vm((n_hp, rows // 2, dm // n_hp), F32)
        scratch = [
            vm((steps, batch, dm), BF16), pltpu.SMEM((batch,), jnp.int32), pltpu.SMEM((hd // 2,), F32),
            vm((6, dm), F32), vm((hdk,), F32), vm((hdk,), F32), vm((n_exp, dm), BF16),
            vm((steps, topk, batch), jnp.int32), vm((rows, topk, n_exp), jnp.int32),
            vm((n_hp, dm, dm // n_hp), BF16), vm((dm, hdk), BF16), vm((dm, hdk), BF16),
            vm((n_hp, group, 2, hd, dm), BF16), vm((batch, hdk, shard), BF16), vm((batch, hdk, shard), BF16),
            vm((fe, dm), BF16), vm((fe, dm), BF16), vm((fe, dm), BF16),
            vm((n_hp, gs_n, batch, LANES), F32), vm((n_hp, steps, batch, LANES), F32), vm((n_hp, steps, batch, LANES), F32),
            vm((rows, heads_kv, hd), F32), vm((batch, qrows, shard), BF16),
            vm((2, n_hp * gs_n + 2, SUBL, LANES), F32), vm((n_hp * gs_n + 2, SUBL, LANES), F32),
            vm((n_hp, gs_n + 2, SUBL, LANES), F32), vm((n_hp + 1, gs_n + 2, SUBL, LANES), F32),
            vm((n, gs_n, SUBL, LANES), F32), vm((2, rows // 2, dm), F32),
            vm((fe // LANES, rows, LANES), F32), vm((fe // LANES, rows, LANES), BF16),
            vm((n_hp, 2, rows // 2, dm // n_hp), F32), qblk, qblk, qblk, blk,
        ] + [vm(o.shape, o.dtype) for o in outs] + [
            dma((14,)), dma((n_hp,)), dma((2,)), dma((1,)), dma((4,)), dma((4,)), dma((2,)), dma((1,)), dma((3,)),
            dma((2,)), dma((n_hp - 1,)), dma((n_hp,)), dma((n - 1,)), dma((n,)), dma((n_hp,)), dma((n_hp,)), dma((n_hp - 1,)), dma((n_hp,)), dma((n - 1,)), dma((n,)),
        ]
        made = pl.pallas_call(
            functools.partial(layer_kernel, dims),
            out_shape=outs,
            in_specs=[any_spec] * len(args),
            out_specs=(any_spec,) * 3,
            scratch_shapes=scratch,
            compiler_params=pltpu.CompilerParams(collective_id=0, has_side_effects=True, vmem_limit_bytes=64 * 1024 * 1024),
        )(*args)
        return pl.pallas_call(
            emit_kernel,
            out_shape=outs,
            in_specs=[any_spec] * 3,
            out_specs=(any_spec,) * 3,
            scratch_shapes=[vm(o.shape, o.dtype) for o in outs] + [dma((2, 3))],
        )(*made)

    replicated = P()
    in_specs = (P('dp'), P(None, 'dp'), P('dp', 'kv'), P('dp', 'kv'), P('dp')) + (replicated,) * 13 + (P(None, None, 'kv'), P(None, None, 'kv'), P(None, 'kv'), replicated, P(None, 'dp'), P(None, 'dp'))
    out_specs = (P(None, 'dp'), P('dp'), P('dp'))
    return jax.shard_map(layer_steps, mesh=mesh, in_specs=in_specs, out_specs=out_specs, check_vma=False)
```

time: 61.2 us -> 45.1 us (0.74)
  Pallas kernels: 55.7 us -> 44.3 us
  local copies, waits for them, and re-layouts: 4.67 us -> 0 us
    pallas_call x1 -> x2, Pallas kernels: 55.7 us -> 44.3 us  [the longest x1 42.6 us: layer_steps(): pl.pallas_call(functools.partial(layer_kernel, dims), out_shape=outs, in_...]
    unnamed x3 -> x0, local copies, waits for them, and re-layouts: 4.67 us -> none
where the time goes in v1:
time: 45.1 us; the launch traced here: 45 us
  Pallas kernels  44.3 us (98%)
  between operations  0.65 us (1%)
    pallas_call x1, Pallas kernels, layer_steps(): pl.pallas_call(functools.partial(layer_kernel, dims), out_shape=outs, in_...  42.6 us
    pallas_call x1, Pallas kernels, layer_steps(): pl.pallas_call(emit_kernel, out_shape=outs, in_specs=[any_spec] * 3, out_...  1.71 us

profile of v1, /device:TPU:113, one launch (start us, length us, event | category | flops | bytes accessed | tf_op | source)
XLA Modules:
  0.0 45.0 jit_solution(11948730502209225276)
XLA Ops:
  0.6 42.6 %shard_map.247 = (bf16[3,16,1536]{2,1,0:T(8,128)(2,1)}, bf16[16,3,8,64]{3,2,1,0:T(8,128)(2,1)}, bf16[16,3,8,64]{3,2,1,0:T(8,128)(2,1)}) custom-call(bf16[16,1536]{1,0:T(8,128)(2,1)} %x_first.1, bf16[2,16,1536]{2,1,0:T(8,128)(2,1)} %next_emb.1, bf16[16,512,512]{2,1,0:T(8,128)(2,1)} %bitcast.17, bf16[16,512,512]{2,1,0:T(8,128)(2,1)} %bitcast.18, s32[16]{0:T(128)} %len_hbm.1, ...), custom_call_target="tpu_custom_call" | custom-call | tf_op jit(solution)/shard_map/pallas_call | solution.py:492
  43.3 1.7 %shard_map.248 = (bf16[3,16,1536]{2,1,0:T(8,128)(2,1)}, bf16[16,3,8,64]{3,2,1,0:T(8,128)(2,1)}, bf16[16,3,8,64]{3,2,1,0:T(8,128)(2,1)}) custom-call(bf16[3,16,1536]{2,1,0:T(8,128)(2,1)} %get-tuple-element.6.refs_0_, bf16[16,3,8,64]{3,2,1,0:T(8,128)(2,1)} %get-tuple-element.7.refs_1_, bf16[16,3,8,64]{3,2,1,0:T(8,128)(2,1)} %get-tuple-element.8.refs_2_), custom_call_target="tpu_custom_call" | custom-call | tf_op jit(solution)/shard_map/pallas_call | solution.py:500

commit v2 on v1

--- a/solution.py
+++ b/solution.py
@@ -30,17 +30,16 @@
                  hid_out, tk_out, tv_out,
                  x_s, len_s, lf_s, vec_s, bk_s, bv_s, wr_s, idx_s, mask_s,
                  wq_s, wk_s, wv_s, wo_s, k_s, v_s, wg_s, wu_s, wd_s,
-                 q_s, kt_s, vt_s, hs_s, p_s, msg_s, pair_s, amsg_s, recv_s, obuf_s, xm_s, gex_s, u_s, pbuf_s, ppair_s, psum_s, rbuf_s, ybuf_s,
+                 q_s, kt_s, vt_s, hs_s, p_s, msg_s, pair_s, tail_s, recv_s, of_s, xm_s, gex_s, u_s, pbuf_s, ppair_s, psum_s, rbuf_s, ybuf_s,
                  hid_s, tk_s, tv_s,
                  small_sem, wq_sem, wkv_sem, wo_sem, k_sem, v_sem, exp_sem, wd_sem, out_sem,
-                 pair_sem, a_send, a_recv, o_send, o_recv, d_send, d_recv, p_send, p_recv, y_send, y_recv):
+                 pair_send, pair_recv, g_send, g_recv, d_send, d_recv, p_send, p_recv, y_send, y_recv):
     n, steps, batch, heads_kv, hd, group, shard, n_exp, ff, dm = dims
     rows = steps * batch
     gs_n = group * steps
     qrows = (gs_n + 1) * heads_kv
     hdk = heads_kv * hd
     n_hp = hdk // LANES
-    half_b = batch // 2
     me = lax.axis_index('kv')
     chip = me // 2
     core = lax.rem(me, 2)
@@ -67,14 +66,11 @@
     for d in range(1, n):
         pl.semaphore_signal(barrier, inc=1, device_id={'kv': lax.rem(me + d, n)}, device_id_type=mesh_id)
 
-    quad = half_b // 2
+    quad = SUBL // 2
     n_quad = batch // quad
 
-    def quad_base(i):
-        return pl.multiple_of((other if i < n_quad // 2 else core) * half_b + (i % 2) * quad, quad)
-
     def cache_copy(src, dst, sem, i):
-        sl = pl.ds(quad_base(i), quad)
+        sl = pl.ds(i * quad, quad)
         return pltpu.make_async_copy(src.at[sl], dst.at[sl], sem.at[i])
 
     k_copies = [cache_copy(k_hbm, k_s, k_sem, i) for i in range(n_quad)]
@@ -153,19 +149,57 @@
     tpos = me * shard + lax.broadcasted_iota(jnp.int32, (1, shard), 1)
     diag = lax.broadcasted_iota(jnp.int32, (heads_kv, hdk), 0) == lax.broadcasted_iota(jnp.int32, (heads_kv, hdk), 1) // hd
     ident = lax.broadcasted_iota(jnp.int32, (qrows, LANES), 0) == lax.broadcasted_iota(jnp.int32, (qrows, LANES), 1)
-    m_slot = n_hp * gs_n
+    o_rows = gs_n * quad
+    last = o_rows // SUBL * SUBL
+    n_tile = last // SUBL + 1
+    lane8 = lax.broadcasted_iota(jnp.int32, (SUBL, LANES), 1)
+    sub8 = lax.broadcasted_iota(jnp.int32, (SUBL, LANES), 0)
+    low8 = lane8 < hd
+    low4 = sub8 < quad
+
+    tail_hp = 2 * core + lax.rem(chip, 2)
+    tail_q = chip // 2 * 2
+    brow = pl.ds(pl.multiple_of(tail_q * quad, SUBL), SUBL)
+    for q in range(n_quad):
+        tail_s[q, :o_rows] = jnp.zeros((o_rows, LANES), F32)
+        tail_s[q, o_rows:o_rows + quad] = jnp.full((quad, LANES), NEG_FILL, F32)
+        tail_s[q, o_rows + quad:] = jnp.zeros((SUBL, LANES), F32)
+    m_tail = jnp.full((SUBL, LANES), NEG_FILL, F32)
+    l_tail = jnp.zeros((SUBL, LANES), F32)
+    for gs in range(gs_n):
+        s = gs % steps
+        qt = q_s[tail_hp, gs, brow, :]
+        cols = []
+        for slot in range(s + 1):
+            prod = qt * kt_s[tail_hp, slot, brow, :]
+            lo = jnp.sum(jnp.where(low8, prod, 0.0), axis=1, keepdims=True)
+            hi = jnp.sum(jnp.where(low8, 0.0, prod), axis=1, keepdims=True)
+            cols.append(jnp.where(low8, lo, hi) * (hd ** -0.5))
+        mx = functools.reduce(jnp.maximum, cols)
+        ws = [jnp.exp(c - mx) for c in cols]
+        lsum = functools.reduce(jnp.add, ws)
+        acc = functools.reduce(jnp.add, [w.astype(BF16).astype(F32) * vt_s[tail_hp, slot, brow, :] for slot, w in enumerate(ws)])
+        for i in range(2):
+            tail_s[tail_q + i, gs * quad:(gs + 1) * quad] = acc[i * quad:(i + 1) * quad]
+        for j in range(2):
+            sel = lane8 == gs * heads_kv + j
+            m_tail = jnp.where(sel, mx[:, j * hd:j * hd + 1], m_tail)
+            l_tail = jnp.where(sel, lsum[:, j * hd:j * hd + 1], l_tail)
+    m_tail = pltpu.roll(m_tail, 2 * tail_hp, 1)
+    l_tail = pltpu.roll(l_tail, 2 * tail_hp, 1)
+    for i in range(2):
+        tail_s[tail_q + i, o_rows:o_rows + quad] = m_tail[i * quad:(i + 1) * quad]
+        tail_s[tail_q + i, o_rows + SUBL:] = l_tail[i * quad:(i + 1) * quad]
 
     def to_row(col):
         return jnp.sum(jnp.where(ident, col, 0.0), axis=0, keepdims=True)
 
     def scores(i):
-        base = quad_base(i)
-        half = other if i < n_quad // 2 else core
         for j in range(quad):
-            b = base + j
+            b = i * quad + j
             blocks = []
             for gs in range(gs_n):
-                qrow = jnp.concatenate([q_s[hp, gs, pl.ds(b, 1), :] for hp in range(n_hp)], axis=1)
+                qrow = jnp.concatenate([q_s[hp, gs, b:b + 1, :] for hp in range(n_hp)], axis=1)
                 blocks.append(jnp.where(diag, qrow, 0.0))
             blocks.append(jnp.zeros((heads_kv, hdk), F32))
             qbd = jnp.concatenate(blocks, axis=0).astype(BF16)
@@ -175,24 +209,90 @@
             m = jnp.max(sc, axis=1, keepdims=True)
             w = jnp.where(keep, jnp.exp(sc - m), 0.0)
             p_s[b] = w.astype(BF16)
-            b8 = (i % 2) * quad + j
-            msg_s[half, m_slot, b8:b8 + 1, :] = to_row(m)
-            msg_s[half, m_slot + 1, b8:b8 + 1, :] = to_row(jnp.sum(w, axis=1, keepdims=True))
+            mrow, lrow = to_row(m), to_row(jnp.sum(w, axis=1, keepdims=True))
+            for hp in range(n_hp):
+                msg_s[i, hp, o_rows + j:o_rows + j + 1, :] = lrow if hp % 2 else mrow
 
     def outputs(i):
-        base = quad_base(i)
-        half = other if i < n_quad // 2 else core
         for j in range(quad):
-            b = base + j
+            b = i * quad + j
             o = lax.dot_general(p_s[b], v_s[b], NT, preferred_element_type=F32)
-            b8 = (i % 2) * quad + j
             for gs in range(gs_n):
                 row = jnp.sum(jnp.where(diag, o[gs * heads_kv:(gs + 1) * heads_kv], 0.0), axis=0, keepdims=True)
                 for hp in range(n_hp):
-                    msg_s[half, hp * gs_n + gs, b8:b8 + 1, :] = row[:, hp * LANES:(hp + 1) * LANES]
+                    msg_s[i, hp, gs * quad + j:gs * quad + j + 1, :] = row[:, hp * LANES:(hp + 1) * LANES]
+
+    def spread(t, lane):
+        return jnp.where(low8, t[:, lane:lane + 1], t[:, lane + 1:lane + 2])
+
+    def both_halves(t):
+        return jnp.where(low4, pltpu.roll(t, quad, 0), pltpu.roll(t, LANES - heads_kv, 1))
 
     sends = []
-    pair_cp = remote(msg_s.at[other], pair_s, pair_sem.at[0], pair_sem.at[1], partner)
+    tiles = [pl.ds(t * SUBL, SUBL) for t in range(n_tile)]
+
+    def pair_start(q):
+        cp = remote(msg_s.at[q, pl.ds(2 * other, 2)], pair_s.at[q], pair_send.at[q], pair_recv.at[q], partner)
+        cp.start()
+        sends.append(cp)
+
+    def pair_merge(q):
+        remote(pair_s.at[q], pair_s.at[q], pair_send.at[q], pair_recv.at[q], partner).wait_recv()
+        own = [msg_s.at[q, 2 * core + k] for k in range(2)]
+        ms = [own[0][tiles[-1]], pair_s[q, 0, tiles[-1]], tail_s[q, tiles[-1]]]
+        ls = [own[1][tiles[-1]], pair_s[q, 1, tiles[-1]], tail_s[q, pl.ds(last + SUBL, SUBL)]]
+        mm = functools.reduce(jnp.maximum, ms)
+        es = [jnp.exp(m - mm) for m in ms]
+        ll = functools.reduce(jnp.add, [e * l for e, l in zip(es, ls)])
+        es = [both_halves(e) for e in es]
+        dst = recv_s.at[q, chip, core]
+        for k in range(2):
+            shift = lax.rem(LANES - 2 * (2 * core + k), LANES)
+            ra, rb = pltpu.roll(es[0], shift, 1), pltpu.roll(es[1], shift, 1)
+            for t in range(n_tile):
+                lane = t * 2 * heads_kv
+                dst[k, tiles[t]] = spread(ra, lane) * own[k][tiles[t]] + spread(rb, lane) * pair_s[q, k, tiles[t]]
+        rt = pltpu.roll(es[2], lax.rem(LANES - 2 * tail_hp, LANES), 1)
+        kt = lax.rem(chip, 2)
+        for t in range(n_tile):
+            dst[kt, tiles[t]] = dst[kt, tiles[t]] + spread(rt, t * 2 * heads_kv) * tail_s[q, tiles[t]]
+        dst[0, o_rows:] = mm[quad:]
+        dst[1, o_rows:] = ll[quad:]
+        for dx in (2, 1, 3):
+            remote(dst, dst, g_send.at[0], g_recv.at[q, chip, core], lax.rem(chip + dx, n_hp) * 2 + core).start()
+        remote(dst, dst, g_send.at[1], g_recv.at[q, chip, core], partner).start()
+
+    def part_arrived(q, cx, c):
+        blk = recv_s.at[q, cx, c]
+        remote(blk, blk, g_send.at[0], g_recv.at[q, cx, c], me).wait_recv()
+        return blk
+
+    def part_relay(q):
+        for dx in (1, 3, 2):
+            cx = lax.rem(chip + dx, n_hp)
+            blk = part_arrived(q, cx, core)
+            remote(blk, blk, g_send.at[1], g_recv.at[q, cx, core], partner).start()
+
+    def final_merge(q):
+        for dx in (0, 1, 3, 2):
+            part_arrived(q, lax.rem(chip + dx, n_hp), other)
+        for c in range(2):
+            ms = [recv_s[q, cx, c, 0, tiles[-1]] for cx in range(n_hp)]
+            mm = functools.reduce(jnp.maximum, ms)
+            es = [jnp.exp(m - mm) for m in ms]
+            inv_l = 1.0 / functools.reduce(jnp.add, [e * recv_s[q, cx, c, 1, tiles[-1]] for cx, e in enumerate(es)])
+            es = [both_halves(e * inv_l) for e in es]
+            for k in range(2):
+                hp = 2 * c + k
+                for t in range(n_tile):
+                    lane = t * 2 * heads_kv + 2 * hp
+                    o = functools.reduce(jnp.add, [spread(e, lane) * recv_s[q, cx, c, k, tiles[t]] for cx, e in enumerate(es)])
+                    for i in range(2):
+                        gs = 2 * t + i
+                        if gs < gs_n:
+                            r = gs % steps * batch + q * quad
+                            of_s[gs // steps, r:r + quad, hp * LANES:(hp + 1) * LANES] = o[i * quad:(i + 1) * quad]
+
     for i in range(n_quad + 1):
         if i < n_quad:
             k_copies[i].wait()
@@ -202,66 +302,18 @@
             scores(i)
         if i:
             outputs(i - 1)
+            if i == 1:
+                pl.semaphore_wait(barrier, n - 1)
+            pair_start(i - 1)
         if i == n_quad // 2:
-            pl.semaphore_wait(barrier, n - 1)
-            pair_cp.start()
             for g in range(group):
                 pltpu.make_async_copy(wo_hbm.at[:, :, g], wo_s.at[:, g], wo_sem.at[0]).start()
             weight_start(wg_hbm, wg_s, exp_sem.at[0])
             weight_start(wu_hbm, wu_s, exp_sem.at[1])
             weight_start(wd_hbm, wd_s, wd_sem.at[0])
-    pair_cp.wait_recv()
-
-    lane8 = lax.broadcasted_iota(jnp.int32, (half_b, LANES), 1)
-    low8 = lane8 < hd
-
-    def spread(t, gs):
-        lane = gs * heads_kv
-        return jnp.where(low8, t[:, lane:lane + 1], t[:, lane + 1:lane + 2])
-
-    ma, mb = msg_s[core, m_slot], pair_s[m_slot]
-    mm = jnp.maximum(ma, mb)
-    ea, eb = jnp.exp(ma - mm), jnp.exp(mb - mm)
-    ll = ea * msg_s[core, m_slot + 1] + eb * pair_s[m_slot + 1]
-    far = (2, 1, 3, 0)
-    for dx in far:
-        hp = lax.rem(chip + dx, n_hp)
-        shift = lax.rem(LANES - 2 * hp, LANES)
-        ra, rb = pltpu.roll(ea, shift, 1), pltpu.roll(eb, shift, 1)
-        dst = recv_s.at[chip] if dx == 0 else amsg_s.at[dx]
-        for gs in range(gs_n):
-            dst[gs] = spread(ra, gs) * msg_s[core, hp * gs_n + gs] + spread(rb, gs) * pair_s[hp * gs_n + gs]
-        dst[gs_n] = pltpu.roll(mm, shift, 1)
-        dst[gs_n + 1] = pltpu.roll(ll, shift, 1)
-    for k, dx in enumerate(far[:-1]):
-        cp = remote(amsg_s.at[dx], recv_s.at[chip], a_send.at[k], a_recv.at[chip], lax.rem(chip + dx, n_hp) * 2 + core)
-        cp.start()
-        sends.append(cp)
-
-    pair_cp.wait_send()
-    brow = pl.ds(pl.multiple_of(core * half_b, half_b), half_b)
-    m_tail = jnp.full((half_b, LANES), NEG_FILL, F32)
-    l_tail = jnp.zeros((half_b, LANES), F32)
-    for gs in range(gs_n):
-        s = gs % steps
-        qt = q_s[chip, gs, brow, :]
-        cols = []
-        for slot in range(s + 1):
-            prod = qt * kt_s[chip, slot, brow, :]
-            lo = jnp.sum(jnp.where(low8, prod, 0.0), axis=1, keepdims=True)
-            hi = jnp.sum(jnp.where(low8, 0.0, prod), axis=1, keepdims=True)
-            cols.append(jnp.where(low8, lo, hi) * (hd ** -0.5))
-        mx = functools.reduce(jnp.maximum, cols)
-        ws = [jnp.exp(c - mx) for c in cols]
-        lsum = functools.reduce(jnp.add, ws)
-        acc = functools.reduce(jnp.add, [w.astype(BF16).astype(F32) * vt_s[chip, slot, brow, :] for slot, w in enumerate(ws)])
-        recv_s[n_hp, gs] = acc
-        for j in range(2):
-            sel = lane8 == gs * heads_kv + j
-            m_tail = jnp.where(sel, mx[:, j * hd:j * hd + 1], m_tail)
-            l_tail = jnp.where(sel, lsum[:, j * hd:j * hd + 1], l_tail)
-    recv_s[n_hp, gs_n] = m_tail
-    recv_s[n_hp, gs_n + 1] = l_tail
+        if i > 1:
+            pair_merge(i - 2)
+    pair_merge(n_quad - 1)
 
     for src_s, dst, out, i in ((kt_s, tk_s, tk_out, 0), (vt_s, tv_s, tv_out, 1)):
         for hp in range(n_hp):
@@ -272,17 +324,16 @@
             dst[:, s] = hs_s[s * batch:(s + 1) * batch].astype(BF16)
         pltpu.make_async_copy(dst, out, out_sem.at[i]).start()
 
-    for dx in (1, 3, 2):
-        src = lax.rem(chip + dx, n_hp)
-        remote(recv_s.at[src], recv_s.at[src], a_send.at[0], a_recv.at[src], me).wait_recv()
-    srcs = range(n_hp + 1)
-    ms = [recv_s[src, gs_n] for src in srcs]
-    mx = functools.reduce(jnp.maximum, ms)
-    al = [jnp.exp(m - mx) for m in ms]
-    tot = functools.reduce(jnp.add, [a * recv_s[src, gs_n + 1] for src, a in zip(srcs, al)])
-    for gs in range(gs_n):
-        acc = functools.reduce(jnp.add, [spread(a, gs) * recv_s[src, gs] for src, a in zip(srcs, al)])
-        obuf_s[me, gs] = (acc / spread(tot, gs)).astype(BF16).astype(F32)
+    part_relay(0)
+    for q in range(n_quad):
+        if q + 1 < n_quad:
+            part_relay(q + 1)
+        else:
+            weight_wait(wo_s, wo_sem.at[0])
+            weight_wait(wg_s, exp_sem.at[0])
+            weight_wait(wu_s, exp_sem.at[1])
+            weight_wait(wd_s, wd_sem.at[0])
+        final_merge(q)
 
     order = (1, 3, 2)
 
@@ -303,30 +354,8 @@
         cp.start()
         sends.append(cp)
 
-    gather_start(obuf_s, o_send, o_recv)
-    weight_wait(wo_s, wo_sem.at[0])
-    weight_wait(wg_s, exp_sem.at[0])
-    weight_wait(wu_s, exp_sem.at[1])
-    weight_wait(wd_s, wd_sem.at[0])
-
-    def wo_part(cx):
-        pieces = []
-        for g in range(group):
-            pieces.append(jnp.concatenate([obuf_s[cx * 2 + half, g * steps + s] for s in range(steps) for half in range(2)], axis=0))
-        lhs = jnp.concatenate(pieces, axis=1).astype(BF16)
-        return jnp.dot(lhs, wo_s[cx].reshape(group * LANES, dm), preferred_element_type=F32)
-
-    arrived(obuf_s, o_send, o_recv, partner)
-    acc = wo_part(chip)
-    for i, dx in enumerate(order):
-        relay(obuf_s, o_send, o_recv, i, dx)
-        if i:
-            cx = lax.rem(chip + order[i - 1], n_hp)
-            arrived(obuf_s, o_send, o_recv, cx * 2 + other)
-            acc = acc + wo_part(cx)
-    cx = lax.rem(chip + order[-1], n_hp)
-    arrived(obuf_s, o_send, o_recv, cx * 2 + other)
-    acc = acc + wo_part(cx)
+    lhs = jnp.concatenate([of_s[g, :, hp * LANES:(hp + 1) * LANES] for hp in range(n_hp) for g in range(group)], axis=1).astype(BF16)
+    acc = jnp.dot(lhs, wo_s[...].reshape(dm, dm), preferred_element_type=F32)
     x = x_s[...].reshape(rows, dm).astype(F32)
     xm = (x + acc + bo).astype(BF16).astype(F32)
     xm_s[...] = xm.reshape(2, rows // 2, dm)
@@ -411,6 +440,8 @@
     hid_cp.start()
     for cp in sends:
         cp.wait_send()
+    for i, blks in enumerate((recv_s.at[pl.ds(0, n_quad - 1), :, pl.ds(0, 1)], recv_s.at[:, :, pl.ds(0, 1)])):
+        pltpu.make_async_copy(blks, blks, g_send.at[i]).wait()
     pltpu.make_async_copy(tk_s, tk_out, out_sem.at[0]).wait()
     pltpu.make_async_copy(tv_s, tv_out, out_sem.at[1]).wait()
     hid_cp.wait()
@@ -469,6 +500,8 @@
             jax.ShapeDtypeStruct((batch, steps, heads_kv, hd), BF16),
             jax.ShapeDtypeStruct((batch, steps, heads_kv, hd), BF16),
         )
+        n_quad = batch // (SUBL // 2)
+        m_rows = (gs_n + 1) * (SUBL // 2)
         blk = vm((n, rows // 2, dm // n_hp), F32)
         qblk = vm((n_hp, rows // 2, dm // n_hp), F32)
         scratch = [
@@ -480,14 +513,13 @@
             vm((fe, dm), BF16), vm((fe, dm), BF16), vm((fe, dm), BF16),
             vm((n_hp, gs_n, batch, LANES), F32), vm((n_hp, steps, batch, LANES), F32), vm((n_hp, steps, batch, LANES), F32),
             vm((rows, heads_kv, hd), F32), vm((batch, qrows, shard), BF16),
-            vm((2, n_hp * gs_n + 2, SUBL, LANES), F32), vm((n_hp * gs_n + 2, SUBL, LANES), F32),
-            vm((n_hp, gs_n + 2, SUBL, LANES), F32), vm((n_hp + 1, gs_n + 2, SUBL, LANES), F32),
-            vm((n, gs_n, SUBL, LANES), F32), vm((2, rows // 2, dm), F32),
+            vm((n_quad, n_hp, m_rows, LANES), F32), vm((n_quad, 2, m_rows, LANES), F32), vm((n_quad, m_rows + SUBL, LANES), F32),
+            vm((n_quad, n_hp, 2, 2, m_rows, LANES), F32), vm((group, rows, hdk), F32), vm((2, rows // 2, dm), F32),
             vm((fe // LANES, rows, LANES), F32), vm((fe // LANES, rows, LANES), BF16),
             vm((n_hp, 2, rows // 2, dm // n_hp), F32), qblk, qblk, qblk, blk,
         ] + [vm(o.shape, o.dtype) for o in outs] + [
             dma((14,)), dma((n_hp,)), dma((2,)), dma((1,)), dma((4,)), dma((4,)), dma((2,)), dma((1,)), dma((3,)),
-            dma((2,)), dma((n_hp - 1,)), dma((n_hp,)), dma((n - 1,)), dma((n,)), dma((n_hp,)), dma((n_hp,)), dma((n_hp - 1,)), dma((n_hp,)), dma((n - 1,)), dma((n,)),
+            dma((n_quad,)), dma((n_quad,)), dma((2,)), dma((n_quad, n_hp, 2)), dma((n_hp,)), dma((n_hp,)), dma((n_hp - 1,)), dma((n_hp,)), dma((n - 1,)), dma((n,)),
         ]
         made = pl.pallas_call(
             functools.partial(layer_kernel, dims),

time: 45.1 us -> 43.9 us (0.973)
  Pallas kernels: 44.3 us -> 43.2 us
    pallas_call x1, Pallas kernels: 42.6 us -> 41.5 us  [layer_steps(): pl.pallas_call(functools.partial(layer_kernel, dims), out_shape=outs, in_...]
where the time goes in v2:
time: 43.9 us; the launch traced here: 43.8 us
  Pallas kernels  43.2 us (98%)
  between operations  0.65 us (1%)
    pallas_call x1, Pallas kernels, layer_steps(): pl.pallas_call(functools.partial(layer_kernel, dims), out_shape=outs, in_...  41.5 us
    pallas_call x1, Pallas kernels, layer_steps(): pl.pallas_call(emit_kernel, out_shape=outs, in_specs=[any_spec] * 3, out_...  1.71 us

profile of v2, /device:TPU:113, one launch (start us, length us, event | category | flops | bytes accessed | tf_op | source)
XLA Modules:
  0.0 43.8 jit_solution(5491780381770736214)
XLA Ops:
  0.6 41.5 %shard_map.247 = (bf16[3,16,1536]{2,1,0:T(8,128)(2,1)}, bf16[16,3,8,64]{3,2,1,0:T(8,128)(2,1)}, bf16[16,3,8,64]{3,2,1,0:T(8,128)(2,1)}) custom-call(bf16[16,1536]{1,0:T(8,128)(2,1)} %x_first.1, bf16[2,16,1536]{2,1,0:T(8,128)(2,1)} %next_emb.1, bf16[16,512,512]{2,1,0:T(8,128)(2,1)} %bitcast.17, bf16[16,512,512]{2,1,0:T(8,128)(2,1)} %bitcast.18, s32[16]{0:T(128)} %len_hbm.1, ...), custom_call_target="tpu_custom_call" | custom-call | tf_op jit(solution)/shard_map/pallas_call | solution.py:524
  42.1 1.7 %shard_map.248 = (bf16[3,16,1536]{2,1,0:T(8,128)(2,1)}, bf16[16,3,8,64]{3,2,1,0:T(8,128)(2,1)}, bf16[16,3,8,64]{3,2,1,0:T(8,128)(2,1)}) custom-call(bf16[3,16,1536]{2,1,0:T(8,128)(2,1)} %get-tuple-element.6.refs_0_, bf16[16,3,8,64]{3,2,1,0:T(8,128)(2,1)} %get-tuple-element.7.refs_1_, bf16[16,3,8,64]{3,2,1,0:T(8,128)(2,1)} %get-tuple-element.8.refs_2_), custom_call_target="tpu_custom_call" | custom-call | tf_op jit(solution)/shard_map/pallas_call | solution.py:532

commit v3 on v2

--- a/solution.py
+++ b/solution.py
@@ -30,10 +30,10 @@
                  hid_out, tk_out, tv_out,
                  x_s, len_s, lf_s, vec_s, bk_s, bv_s, wr_s, idx_s, mask_s,
                  wq_s, wk_s, wv_s, wo_s, k_s, v_s, wg_s, wu_s, wd_s,
-                 q_s, kt_s, vt_s, hs_s, p_s, msg_s, pair_s, tail_s, recv_s, of_s, xm_s, gex_s, u_s, pbuf_s, ppair_s, psum_s, rbuf_s, ybuf_s,
+                 q_s, kt_s, vt_s, hs_s, p_s, msg_s, pair_s, ml_s, mlp_s, cf_s, tail_s, recv_s, of_s, xm_s, gex_s, u_s, pbuf_s, ppair_s, psum_s, rbuf_s, ybuf_s,
                  hid_s, tk_s, tv_s,
                  small_sem, wq_sem, wkv_sem, wo_sem, k_sem, v_sem, exp_sem, wd_sem, out_sem,
-                 pair_send, pair_recv, g_send, g_recv, d_send, d_recv, p_send, p_recv, y_send, y_recv):
+                 ml_send, ml_recv, pair_send, pair_recv, g_send, g_recv, d_send, d_recv, p_send, p_recv, y_send, y_recv):
     n, steps, batch, heads_kv, hd, group, shard, n_exp, ff, dm = dims
     rows = steps * batch
     gs_n = group * steps
@@ -150,6 +150,7 @@
     diag = lax.broadcasted_iota(jnp.int32, (heads_kv, hdk), 0) == lax.broadcasted_iota(jnp.int32, (heads_kv, hdk), 1) // hd
     ident = lax.broadcasted_iota(jnp.int32, (qrows, LANES), 0) == lax.broadcasted_iota(jnp.int32, (qrows, LANES), 1)
     o_rows = gs_n * quad
+    m_rows = o_rows + quad
     last = o_rows // SUBL * SUBL
     n_tile = last // SUBL + 1
     lane8 = lax.broadcasted_iota(jnp.int32, (SUBL, LANES), 1)
@@ -161,9 +162,11 @@
     tail_q = chip // 2 * 2
     brow = pl.ds(pl.multiple_of(tail_q * quad, SUBL), SUBL)
     for q in range(n_quad):
-        tail_s[q, :o_rows] = jnp.zeros((o_rows, LANES), F32)
-        tail_s[q, o_rows:o_rows + quad] = jnp.full((quad, LANES), NEG_FILL, F32)
-        tail_s[q, o_rows + quad:] = jnp.zeros((SUBL, LANES), F32)
+        tail_s[q, :m_rows] = jnp.zeros((m_rows, LANES), F32)
+        tail_s[q, m_rows:m_rows + SUBL] = jnp.full((SUBL, LANES), NEG_FILL, F32)
+        tail_s[q, m_rows + SUBL:] = jnp.zeros((SUBL, LANES), F32)
+        for hp in range(n_hp):
+            msg_s[q, hp, o_rows:] = jnp.zeros((quad, LANES), F32)
     m_tail = jnp.full((SUBL, LANES), NEG_FILL, F32)
     l_tail = jnp.zeros((SUBL, LANES), F32)
     for gs in range(gs_n):
@@ -188,8 +191,11 @@
     m_tail = pltpu.roll(m_tail, 2 * tail_hp, 1)
     l_tail = pltpu.roll(l_tail, 2 * tail_hp, 1)
     for i in range(2):
-        tail_s[tail_q + i, o_rows:o_rows + quad] = m_tail[i * quad:(i + 1) * quad]
-        tail_s[tail_q + i, o_rows + SUBL:] = l_tail[i * quad:(i + 1) * quad]
+        for k in range(2):
+            rs = slice(m_rows + k * quad, m_rows + (k + 1) * quad)
+            tail_s[tail_q + i, rs] = m_tail[i * quad:(i + 1) * quad]
+            rs = slice(m_rows + SUBL + k * quad, m_rows + SUBL + (k + 1) * quad)
+            tail_s[tail_q + i, rs] = l_tail[i * quad:(i + 1) * quad]
 
     def to_row(col):
         return jnp.sum(jnp.where(ident, col, 0.0), axis=0, keepdims=True)
@@ -210,8 +216,10 @@
             w = jnp.where(keep, jnp.exp(sc - m), 0.0)
             p_s[b] = w.astype(BF16)
             mrow, lrow = to_row(m), to_row(jnp.sum(w, axis=1, keepdims=True))
-            for hp in range(n_hp):
-                msg_s[i, hp, o_rows + j:o_rows + j + 1, :] = lrow if hp % 2 else mrow
+            for k in range(2):
+                r = k * quad + j
+                ml_s[i, 0, r:r + 1, :] = mrow
+                ml_s[i, 1, r:r + 1, :] = lrow
 
     def outputs(i):
         for j in range(quad):
@@ -226,38 +234,39 @@
         return jnp.where(low8, t[:, lane:lane + 1], t[:, lane + 1:lane + 2])
 
     def both_halves(t):
-        return jnp.where(low4, pltpu.roll(t, quad, 0), pltpu.roll(t, LANES - heads_kv, 1))
-
-    sends = []
+        return jnp.where(low4, t, pltpu.roll(t, LANES - heads_kv, 1))
+
     tiles = [pl.ds(t * SUBL, SUBL) for t in range(n_tile)]
 
-    def pair_start(q):
-        cp = remote(msg_s.at[q, pl.ds(2 * other, 2)], pair_s.at[q], pair_send.at[q], pair_recv.at[q], partner)
-        cp.start()
-        sends.append(cp)
-
-    def pair_merge(q):
-        remote(pair_s.at[q], pair_s.at[q], pair_send.at[q], pair_recv.at[q], partner).wait_recv()
-        own = [msg_s.at[q, 2 * core + k] for k in range(2)]
-        ms = [own[0][tiles[-1]], pair_s[q, 0, tiles[-1]], tail_s[q, tiles[-1]]]
-        ls = [own[1][tiles[-1]], pair_s[q, 1, tiles[-1]], tail_s[q, pl.ds(last + SUBL, SUBL)]]
+    def ml_copy(q):
+        return remote(ml_s.at[q], mlp_s.at[q], ml_send.at[0], ml_recv.at[q], partner)
+
+    def pair_copy(q):
+        return remote(msg_s.at[q, pl.ds(2 * other, 2)], pair_s.at[q], pair_send.at[0], pair_recv.at[q], partner)
+
+    def pair_factors(q):
+        ms = [ml_s[q, 0], mlp_s[q, 0], tail_s[q, pl.ds(m_rows, SUBL)]]
+        ls = [ml_s[q, 1], mlp_s[q, 1], tail_s[q, pl.ds(m_rows + SUBL, SUBL)]]
         mm = functools.reduce(jnp.maximum, ms)
         es = [jnp.exp(m - mm) for m in ms]
         ll = functools.reduce(jnp.add, [e * l for e, l in zip(es, ls)])
+        recv_s[q, chip, core, 0, o_rows:] = mm[quad:]
+        recv_s[q, chip, core, 1, o_rows:] = ll[quad:]
         es = [both_halves(e) for e in es]
+        es[2] = pltpu.roll(es[2], lax.rem(LANES - 2 * tail_hp, LANES), 1)
+        for k in range(2):
+            shift = lax.rem(LANES - 2 * (2 * core + k), LANES)
+            fs = [pltpu.roll(es[0], shift, 1), pltpu.roll(es[1], shift, 1), jnp.where(lax.rem(chip, 2) == k, es[2], 0.0)]
+            for i, f in enumerate(fs):
+                for t in range(n_tile):
+                    cf_s[q, k, i, tiles[t]] = spread(f, t * 2 * heads_kv)
+
+    def pair_merge(q):
+        pair_copy(q).wait_recv()
         dst = recv_s.at[q, chip, core]
         for k in range(2):
-            shift = lax.rem(LANES - 2 * (2 * core + k), LANES)
-            ra, rb = pltpu.roll(es[0], shift, 1), pltpu.roll(es[1], shift, 1)
-            for t in range(n_tile):
-                lane = t * 2 * heads_kv
-                dst[k, tiles[t]] = spread(ra, lane) * own[k][tiles[t]] + spread(rb, lane) * pair_s[q, k, tiles[t]]
-        rt = pltpu.roll(es[2], lax.rem(LANES - 2 * tail_hp, LANES), 1)
-        kt = lax.rem(chip, 2)
-        for t in range(n_tile):
-            dst[kt, tiles[t]] = dst[kt, tiles[t]] + spread(rt, t * 2 * heads_kv) * tail_s[q, tiles[t]]
-        dst[0, o_rows:] = mm[quad:]
-        dst[1, o_rows:] = ll[quad:]
+            rs = pl.ds(0, o_rows)
+            dst[k, rs] = cf_s[q, k, 0, rs] * msg_s[q, 2 * core + k, rs] + cf_s[q, k, 1, rs] * pair_s[q, k, rs] + cf_s[q, k, 2, rs] * tail_s[q, rs]
         for dx in (2, 1, 3):
             remote(dst, dst, g_send.at[0], g_recv.at[q, chip, core], lax.rem(chip + dx, n_hp) * 2 + core).start()
         remote(dst, dst, g_send.at[1], g_recv.at[q, chip, core], partner).start()
@@ -281,7 +290,7 @@
             mm = functools.reduce(jnp.maximum, ms)
             es = [jnp.exp(m - mm) for m in ms]
             inv_l = 1.0 / functools.reduce(jnp.add, [e * recv_s[q, cx, c, 1, tiles[-1]] for cx, e in enumerate(es)])
-            es = [both_halves(e * inv_l) for e in es]
+            es = [jnp.where(low4, pltpu.roll(e * inv_l, quad, 0), pltpu.roll(e * inv_l, LANES - heads_kv, 1)) for e in es]
             for k in range(2):
                 hp = 2 * c + k
                 for t in range(n_tile):
@@ -298,13 +307,20 @@
             k_copies[i].wait()
         if i:
             v_copies[i - 1].wait()
+        if i > 1:
+            ml_copy(i - 2).wait_recv()
         if i < n_quad:
             scores(i)
         if i:
             outputs(i - 1)
-            if i == 1:
-                pl.semaphore_wait(barrier, n - 1)
-            pair_start(i - 1)
+        if i > 1:
+            pair_factors(i - 2)
+        if i == 0:
+            pl.semaphore_wait(barrier, n - 1)
+        if i < n_quad:
+            ml_copy(i).start()
+        if i:
+            pair_copy(i - 1).start()
         if i == n_quad // 2:
             for g in range(group):
                 pltpu.make_async_copy(wo_hbm.at[:, :, g], wo_s.at[:, g], wo_sem.at[0]).start()
@@ -313,16 +329,9 @@
             weight_start(wd_hbm, wd_s, wd_sem.at[0])
         if i > 1:
             pair_merge(i - 2)
+    ml_copy(n_quad - 1).wait_recv()
+    pair_factors(n_quad - 1)
     pair_merge(n_quad - 1)
-
-    for src_s, dst, out, i in ((kt_s, tk_s, tk_out, 0), (vt_s, tv_s, tv_out, 1)):
-        for hp in range(n_hp):
-            t = src_s[hp].reshape(rows, LANES)
-            hs_s[:, 2 * hp, :] = t[:, :hd]
-            hs_s[:, 2 * hp + 1, :] = pltpu.roll(t, hd, 1)[:, :hd]
-        for s in range(steps):
-            dst[:, s] = hs_s[s * batch:(s + 1) * batch].astype(BF16)
-        pltpu.make_async_copy(dst, out, out_sem.at[i]).start()
 
     part_relay(0)
     for q in range(n_quad):
@@ -334,25 +343,6 @@
             weight_wait(wu_s, exp_sem.at[1])
             weight_wait(wd_s, wd_sem.at[0])
         final_merge(q)
-
-    order = (1, 3, 2)
-
-    def gather_start(buf, send, recv):
-        for i, dx in enumerate((2, 1, 3, 0)):
-            dev = partner if dx == 0 else lax.rem(chip + dx, n_hp) * 2 + core
-            cp = remote(buf.at[me], buf.at[me], send.at[i], recv.at[me], dev)
-            cp.start()
-            sends.append(cp)
-
-    def arrived(buf, send, recv, src):
-        remote(buf.at[src], buf.at[src], send.at[0], recv.at[src], me).wait_recv()
-
-    def relay(buf, send, recv, i, dx):
-        src = lax.rem(chip + dx, n_hp) * 2 + core
-        arrived(buf, send, recv, src)
-        cp = remote(buf.at[src], buf.at[src], send.at[n_hp + i], recv.at[src], partner)
-        cp.start()
-        sends.append(cp)
 
     lhs = jnp.concatenate([of_s[g, :, hp * LANES:(hp + 1) * LANES] for hp in range(n_hp) for g in range(group)], axis=1).astype(BF16)
     acc = jnp.dot(lhs, wo_s[...].reshape(dm, dm), preferred_element_type=F32)
@@ -397,51 +387,75 @@
         return 0
 
     lax.fori_loop(1, n_ec // peel, expert, 0)
-    cw = dm // n_hp
+    cw = n_hp * LANES
+    n_ch = dm // cw
     hr = rows // 2
     u = jnp.concatenate([u_s[c] for c in range(n_ec)], axis=1)
 
-    def add_pair(k, cq, own):
-        remote(ppair_s.at[cq], ppair_s.at[cq], d_send.at[0], d_recv.at[cq], me).wait_recv()
-        tot = pbuf_s[cq, core] + ppair_s[cq]
-        if own:
-            return tot
-        psum_s[cq] = tot
-        cp = remote(psum_s.at[cq], rbuf_s.at[chip], p_send.at[k], p_recv.at[chip], cq * 2 + core)
-        cp.start()
-        sends.append(cp)
-
-    down = (2, 1, 3, 0)
-    for k, dx in enumerate(down):
-        cq = lax.rem(chip + dx, n_hp)
-        cols = pl.ds(pl.multiple_of(cq * cw, LANES), cw)
-        part = jnp.dot(u, wd_s[:, cols], preferred_element_type=F32)
-        pbuf_s[cq] = part.astype(BF16).astype(F32).reshape(2, hr, cw)
-        cp = remote(pbuf_s.at[cq, other], ppair_s.at[cq], d_send.at[k], d_recv.at[cq], partner)
-        cp.start()
-        sends.append(cp)
+    def d_copy(k):
+        return remote(pbuf_s.at[k, other], ppair_s.at[k], d_send.at[0], d_recv.at[k], partner)
+
+    def add_pair(k):
+        d_copy(k).wait_recv()
+        psum_s[k] = pbuf_s[k, core] + ppair_s[k]
+        for dx in (2, 1, 3):
+            cx = lax.rem(chip + dx, n_hp)
+            remote(psum_s.at[k, cx], rbuf_s.at[k, chip], p_send.at[0], p_recv.at[k, chip], cx * 2 + core).start()
+
+    for k in range(n_ch):
+        part = jnp.dot(u, wd_s[:, k * cw:(k + 1) * cw], preferred_element_type=F32)
+        part = part.astype(BF16).astype(F32)
+        for half in range(2):
+            for cx in range(n_hp):
+                pbuf_s[k, half, cx] = part[half * hr:(half + 1) * hr, cx * LANES:(cx + 1) * LANES]
+        d_copy(k).start()
         if k:
-            add_pair(k - 1, lax.rem(chip + down[k - 1], n_hp), False)
-    y = xm_s[core, :, pl.ds(pl.multiple_of(chip * cw, LANES), cw)] + add_pair(0, chip, True)
-    for dx in (1, 3, 2):
-        src = lax.rem(chip + dx, n_hp)
-        remote(rbuf_s.at[src], rbuf_s.at[src], p_send.at[0], p_recv.at[src], me).wait_recv()
-        y = y + rbuf_s[src]
-    ybuf_s[me] = y.astype(BF16).astype(F32)
-    gather_start(ybuf_s, y_send, y_recv)
-    for i, dx in enumerate(order):
-        relay(ybuf_s, y_send, y_recv, i, dx)
-    for dx in (0,) + order:
-        arrived(ybuf_s, y_send, y_recv, lax.rem(chip + dx, n_hp) * 2 + other)
-    for cq in range(n_hp):
-        blk = jnp.concatenate([ybuf_s[cq * 2], ybuf_s[cq * 2 + 1]], axis=0)
-        hid_s[:, :, cq * cw:(cq + 1) * cw] = blk.astype(BF16).reshape(steps, batch, cw)
+            add_pair(k - 1)
+    add_pair(n_ch - 1)
+
+    for src_s, dst, out, i in ((kt_s, tk_s, tk_out, 0), (vt_s, tv_s, tv_out, 1)):
+        for hp in range(n_hp):
+            t = src_s[hp].reshape(rows, LANES)
+            hs_s[:, 2 * hp, :] = t[:, :hd]
+            hs_s[:, 2 * hp + 1, :] = pltpu.roll(t, hd, 1)[:, :hd]
+        for s in range(steps):
+            dst[:, s] = hs_s[s * batch:(s + 1) * batch].astype(BF16)
+        pltpu.make_async_copy(dst, out, out_sem.at[i]).start()
+
+    def y_arrived(k, cx, c):
+        blk = ybuf_s.at[k, cx, c]
+        remote(blk, blk, y_send.at[0], y_recv.at[k, cx, c], me).wait_recv()
+        return blk
+
+    for k in range(n_ch):
+        y = xm_s[core, :, pl.ds(pl.multiple_of(k * cw + chip * LANES, LANES), LANES)] + psum_s[k, chip]
+        for dx in (1, 3, 2):
+            cx = lax.rem(chip + dx, n_hp)
+            remote(rbuf_s.at[k, cx], rbuf_s.at[k, cx], p_send.at[0], p_recv.at[k, cx], me).wait_recv()
+            y = y + rbuf_s[k, cx]
+        ybuf_s[k, chip, core] = y.astype(BF16).astype(F32)
+        blk = ybuf_s.at[k, chip, core]
+        for dx in (2, 1, 3):
+            remote(blk, blk, y_send.at[0], y_recv.at[k, chip, core], lax.rem(chip + dx, n_hp) * 2 + core).start()
+        remote(blk, blk, y_send.at[1], y_recv.at[k, chip, core], partner).start()
+    for k in range(n_ch):
+        for dx in (1, 3, 2):
+            cx = lax.rem(chip + dx, n_hp)
+            blk = y_arrived(k, cx, core)
+            remote(blk, blk, y_send.at[1], y_recv.at[k, cx, core], partner).start()
+    for k in range(n_ch):
+        for dx in (0, 1, 3, 2):
+            y_arrived(k, lax.rem(chip + dx, n_hp), other)
+        for cx in range(n_hp):
+            blk = jnp.concatenate([ybuf_s[k, cx, 0], ybuf_s[k, cx, 1]], axis=0)
+            hid_s[:, :, k * cw + cx * LANES:k * cw + (cx + 1) * LANES] = blk.astype(BF16).reshape(steps, batch, LANES)
     hid_cp = pltpu.make_async_copy(hid_s, hid_out, out_sem.at[2])
     hid_cp.start()
-    for cp in sends:
-        cp.wait_send()
-    for i, blks in enumerate((recv_s.at[pl.ds(0, n_quad - 1), :, pl.ds(0, 1)], recv_s.at[:, :, pl.ds(0, 1)])):
-        pltpu.make_async_copy(blks, blks, g_send.at[i]).wait()
+    one = pl.ds(0, 1)
+    part_blocks = pl.ds(0, n_hp - 1)
+    for blks, sem in ((mlp_s, ml_send.at[0]), (pair_s, pair_send.at[0]), (recv_s.at[part_blocks, :, one], g_send.at[0]), (recv_s.at[:, :, one], g_send.at[1]),
+                      (ppair_s, d_send.at[0]), (rbuf_s.at[:, part_blocks], p_send.at[0]), (ybuf_s.at[:, part_blocks, one], y_send.at[0]), (ybuf_s.at[:, :, one], y_send.at[1])):
+        pltpu.make_async_copy(blks, blks, sem).wait()
     pltpu.make_async_copy(tk_s, tk_out, out_sem.at[0]).wait()
     pltpu.make_async_copy(tv_s, tv_out, out_sem.at[1]).wait()
     hid_cp.wait()
@@ -502,8 +516,8 @@
         )
         n_quad = batch // (SUBL // 2)
         m_rows = (gs_n + 1) * (SUBL // 2)
-        blk = vm((n, rows // 2, dm // n_hp), F32)
-        qblk = vm((n_hp, rows // 2, dm // n_hp), F32)
+        n_ch = dm // hdk
+        qblk = vm((n_ch, n_hp, rows // 2, LANES), F32)
         scratch = [
             vm((steps, batch, dm), BF16), pltpu.SMEM((batch,), jnp.int32), pltpu.SMEM((hd // 2,), F32),
             vm((6, dm), F32), vm((hdk,), F32), vm((hdk,), F32), vm((n_exp, dm), BF16),
@@ -513,13 +527,15 @@
             vm((fe, dm), BF16), vm((fe, dm), BF16), vm((fe, dm), BF16),
             vm((n_hp, gs_n, batch, LANES), F32), vm((n_hp, steps, batch, LANES), F32), vm((n_hp, steps, batch, LANES), F32),
             vm((rows, heads_kv, hd), F32), vm((batch, qrows, shard), BF16),
-            vm((n_quad, n_hp, m_rows, LANES), F32), vm((n_quad, 2, m_rows, LANES), F32), vm((n_quad, m_rows + SUBL, LANES), F32),
+            vm((n_quad, n_hp, m_rows, LANES), F32), vm((n_quad, 2, m_rows, LANES), F32),
+            vm((n_quad, 2, SUBL, LANES), F32), vm((n_quad, 2, SUBL, LANES), F32), vm((n_quad, 2, 3, m_rows, LANES), F32), vm((n_quad, m_rows + 2 * SUBL, LANES), F32),
             vm((n_quad, n_hp, 2, 2, m_rows, LANES), F32), vm((group, rows, hdk), F32), vm((2, rows // 2, dm), F32),
             vm((fe // LANES, rows, LANES), F32), vm((fe // LANES, rows, LANES), BF16),
-            vm((n_hp, 2, rows // 2, dm // n_hp), F32), qblk, qblk, qblk, blk,
+            vm((n_ch, 2, n_hp, rows // 2, LANES), F32), qblk, qblk, qblk, vm((n_ch, n_hp, 2, rows // 2, LANES), F32),
         ] + [vm(o.shape, o.dtype) for o in outs] + [
             dma((14,)), dma((n_hp,)), dma((2,)), dma((1,)), dma((4,)), dma((4,)), dma((2,)), dma((1,)), dma((3,)),
-            dma((n_quad,)), dma((n_quad,)), dma((2,)), dma((n_quad, n_hp, 2)), dma((n_hp,)), dma((n_hp,)), dma((n_hp - 1,)), dma((n_hp,)), dma((n - 1,)), dma((n,)),
+            dma((1,)), dma((n_quad,)), dma((1,)), dma((n_quad,)), dma((2,)), dma((n_quad, n_hp, 2)),
+            dma((1,)), dma((n_ch,)), dma((1,)), dma((n_ch, n_hp)), dma((2,)), dma((n_ch, n_hp, 2)),
         ]
         made = pl.pallas_call(
             functools.partial(layer_kernel, dims),

time: 43.9 us -> 43.4 us (0.989)
  Pallas kernels: 43.2 us -> 42.7 us
    pallas_call x1, Pallas kernels: 41.5 us -> 41 us  [layer_steps(): pl.pallas_call(functools.partial(layer_kernel, dims), out_shape=outs, in_...]
where the time goes in v3:
time: 43.4 us; the launch traced here: 43.3 us
  Pallas kernels  42.7 us (98%)
  between operations  0.65 us (1%)
    pallas_call x1, Pallas kernels, layer_steps(): pl.pallas_call(functools.partial(layer_kernel, dims), out_shape=outs, in_...  41 us
    pallas_call x1, Pallas kernels, layer_steps(): pl.pallas_call(emit_kernel, out_shape=outs, in_specs=[any_spec] * 3, out_...  1.71 us

profile of v3, /device:TPU:113, one launch (start us, length us, event | category | flops | bytes accessed | tf_op | source)
XLA Modules:
  0.0 43.3 jit_solution(11911953242719556256)
XLA Ops:
  0.6 41.0 %shard_map.247 = (bf16[3,16,1536]{2,1,0:T(8,128)(2,1)}, bf16[16,3,8,64]{3,2,1,0:T(8,128)(2,1)}, bf16[16,3,8,64]{3,2,1,0:T(8,128)(2,1)}) custom-call(bf16[16,1536]{1,0:T(8,128)(2,1)} %x_first.1, bf16[2,16,1536]{2,1,0:T(8,128)(2,1)} %next_emb.1, bf16[16,512,512]{2,1,0:T(8,128)(2,1)} %bitcast.17, bf16[16,512,512]{2,1,0:T(8,128)(2,1)} %bitcast.18, s32[16]{0:T(128)} %len_hbm.1, ...), custom_call_target="tpu_custom_call" | custom-call | tf_op jit(solution)/shard_map/pallas_call | solution.py:540
  41.6 1.7 %shard_map.248 = (bf16[3,16,1536]{2,1,0:T(8,128)(2,1)}, bf16[16,3,8,64]{3,2,1,0:T(8,128)(2,1)}, bf16[16,3,8,64]{3,2,1,0:T(8,128)(2,1)}) custom-call(bf16[3,16,1536]{2,1,0:T(8,128)(2,1)} %get-tuple-element.6.refs_0_, bf16[16,3,8,64]{3,2,1,0:T(8,128)(2,1)} %get-tuple-element.7.refs_1_, bf16[16,3,8,64]{3,2,1,0:T(8,128)(2,1)} %get-tuple-element.8.refs_2_), custom_call_target="tpu_custom_call" | custom-call | tf_op jit(solution)/shard_map/pallas_call | solution.py:548

commit v4 on v3

--- a/solution.py
+++ b/solution.py
@@ -307,6 +307,12 @@
             k_copies[i].wait()
         if i:
             v_copies[i - 1].wait()
+        if i == n_quad - 1:
+            for g in range(group):
+                pltpu.make_async_copy(wo_hbm.at[:, :, g], wo_s.at[:, g], wo_sem.at[0]).start()
+            weight_start(wg_hbm, wg_s, exp_sem.at[0])
+            weight_start(wu_hbm, wu_s, exp_sem.at[1])
+            weight_start(wd_hbm, wd_s, wd_sem.at[0])
         if i > 1:
             ml_copy(i - 2).wait_recv()
         if i < n_quad:
@@ -321,12 +327,6 @@
             ml_copy(i).start()
         if i:
             pair_copy(i - 1).start()
-        if i == n_quad // 2:
-            for g in range(group):
-                pltpu.make_async_copy(wo_hbm.at[:, :, g], wo_s.at[:, g], wo_sem.at[0]).start()
-            weight_start(wg_hbm, wg_s, exp_sem.at[0])
-            weight_start(wu_hbm, wu_s, exp_sem.at[1])
-            weight_start(wd_hbm, wd_s, wd_sem.at[0])
         if i > 1:
             pair_merge(i - 2)
     ml_copy(n_quad - 1).wait_recv()
@@ -341,7 +341,6 @@
             weight_wait(wo_s, wo_sem.at[0])
             weight_wait(wg_s, exp_sem.at[0])
             weight_wait(wu_s, exp_sem.at[1])
-            weight_wait(wd_s, wd_sem.at[0])
         final_merge(q)
 
     lhs = jnp.concatenate([of_s[g, :, hp * LANES:(hp + 1) * LANES] for hp in range(n_hp) for g in range(group)], axis=1).astype(BF16)
@@ -402,6 +401,7 @@
             cx = lax.rem(chip + dx, n_hp)
             remote(psum_s.at[k, cx], rbuf_s.at[k, chip], p_send.at[0], p_recv.at[k, chip], cx * 2 + core).start()
 
+    weight_wait(wd_s, wd_sem.at[0])
     for k in range(n_ch):
         part = jnp.dot(u, wd_s[:, k * cw:(k + 1) * cw], preferred_element_type=F32)
         part = part.astype(BF16).astype(F32)

time: 43.4 us -> 43.5 us (level)
  no operation moved by 1% of the time
where the time goes in v4:
time: 43.5 us; the launch traced here: 43.4 us
  Pallas kernels  42.7 us (98%)
  between operations  0.65 us (1%)
    pallas_call x1, Pallas kernels, layer_steps(): pl.pallas_call(functools.partial(layer_kernel, dims), out_shape=outs, in_...  41 us
    pallas_call x1, Pallas kernels, layer_steps(): pl.pallas_call(emit_kernel, out_shape=outs, in_specs=[any_spec] * 3, out_...  1.71 us

profile of v4, /device:TPU:113, one launch (start us, length us, event | category | flops | bytes accessed | tf_op | source)
XLA Modules:
  0.0 43.4 jit_solution(14615618159902942554)
XLA Ops:
  0.6 41.0 %shard_map.247 = (bf16[3,16,1536]{2,1,0:T(8,128)(2,1)}, bf16[16,3,8,64]{3,2,1,0:T(8,128)(2,1)}, bf16[16,3,8,64]{3,2,1,0:T(8,128)(2,1)}) custom-call(bf16[16,1536]{1,0:T(8,128)(2,1)} %x_first.1, bf16[2,16,1536]{2,1,0:T(8,128)(2,1)} %next_emb.1, bf16[16,512,512]{2,1,0:T(8,128)(2,1)} %bitcast.17, bf16[16,512,512]{2,1,0:T(8,128)(2,1)} %bitcast.18, s32[16]{0:T(128)} %len_hbm.1, ...), custom_call_target="tpu_custom_call" | custom-call | tf_op jit(solution)/shard_map/pallas_call | solution.py:540
  41.7 1.7 %shard_map.248 = (bf16[3,16,1536]{2,1,0:T(8,128)(2,1)}, bf16[16,3,8,64]{3,2,1,0:T(8,128)(2,1)}, bf16[16,3,8,64]{3,2,1,0:T(8,128)(2,1)}) custom-call(bf16[3,16,1536]{2,1,0:T(8,128)(2,1)} %get-tuple-element.6.refs_0_, bf16[16,3,8,64]{3,2,1,0:T(8,128)(2,1)} %get-tuple-element.7.refs_1_, bf16[16,3,8,64]{3,2,1,0:T(8,128)(2,1)} %get-tuple-element.8.refs_2_), custom_call_target="tpu_custom_call" | custom-call | tf_op jit(solution)/shard_map/pallas_call | solution.py:548

commit v5 on v4

--- a/solution.py
+++ b/solution.py
@@ -17,6 +17,7 @@
 F32 = jnp.float32
 BF16 = jnp.bfloat16
 NT = (((1,), (1,)), ((), ()))
+VMEM_BYTES = 61 * 1024 * 1024
 
 
 def norm_rows(x, gain, bias):
@@ -31,8 +32,7 @@
                  x_s, len_s, lf_s, vec_s, bk_s, bv_s, wr_s, idx_s, mask_s,
                  wq_s, wk_s, wv_s, wo_s, k_s, v_s, wg_s, wu_s, wd_s,
                  q_s, kt_s, vt_s, hs_s, p_s, msg_s, pair_s, ml_s, mlp_s, cf_s, tail_s, recv_s, of_s, xm_s, gex_s, u_s, pbuf_s, ppair_s, psum_s, rbuf_s, ybuf_s,
-                 hid_s, tk_s, tv_s,
-                 small_sem, wq_sem, wkv_sem, wo_sem, k_sem, v_sem, exp_sem, wd_sem, out_sem,
+                 small_sem, wq_sem, wkv_sem, wo_sem, k_sem, v_sem, exp_sem, wd_sem,
                  ml_send, ml_recv, pair_send, pair_recv, g_send, g_recv, d_send, d_recv, p_send, p_recv, y_send, y_recv):
     n, steps, batch, heads_kv, hd, group, shard, n_exp, ff, dm = dims
     rows = steps * batch
@@ -413,14 +413,13 @@
             add_pair(k - 1)
     add_pair(n_ch - 1)
 
-    for src_s, dst, out, i in ((kt_s, tk_s, tk_out, 0), (vt_s, tv_s, tv_out, 1)):
+    for src_s, dst in ((kt_s, tk_out), (vt_s, tv_out)):
         for hp in range(n_hp):
             t = src_s[hp].reshape(rows, LANES)
             hs_s[:, 2 * hp, :] = t[:, :hd]
             hs_s[:, 2 * hp + 1, :] = pltpu.roll(t, hd, 1)[:, :hd]
         for s in range(steps):
             dst[:, s] = hs_s[s * batch:(s + 1) * batch].astype(BF16)
-        pltpu.make_async_copy(dst, out, out_sem.at[i]).start()
 
     def y_arrived(k, cx, c):
         blk = ybuf_s.at[k, cx, c]
@@ -448,29 +447,19 @@
             y_arrived(k, lax.rem(chip + dx, n_hp), other)
         for cx in range(n_hp):
             blk = jnp.concatenate([ybuf_s[k, cx, 0], ybuf_s[k, cx, 1]], axis=0)
-            hid_s[:, :, k * cw + cx * LANES:k * cw + (cx + 1) * LANES] = blk.astype(BF16).reshape(steps, batch, LANES)
-    hid_cp = pltpu.make_async_copy(hid_s, hid_out, out_sem.at[2])
-    hid_cp.start()
+            hid_out[:, :, k * cw + cx * LANES:k * cw + (cx + 1) * LANES] = blk.astype(BF16).reshape(steps, batch, LANES)
     one = pl.ds(0, 1)
     part_blocks = pl.ds(0, n_hp - 1)
     for blks, sem in ((mlp_s, ml_send.at[0]), (pair_s, pair_send.at[0]), (recv_s.at[part_blocks, :, one], g_send.at[0]), (recv_s.at[:, :, one], g_send.at[1]),
                       (ppair_s, d_send.at[0]), (rbuf_s.at[:, part_blocks], p_send.at[0]), (ybuf_s.at[:, part_blocks, one], y_send.at[0]), (ybuf_s.at[:, :, one], y_send.at[1])):
         pltpu.make_async_copy(blks, blks, sem).wait()
-    pltpu.make_async_copy(tk_s, tk_out, out_sem.at[0]).wait()
-    pltpu.make_async_copy(tv_s, tv_out, out_sem.at[1]).wait()
-    hid_cp.wait()
 
 
 def emit_kernel(*refs):
-    k = len(refs) // 3
-    ins, outs, bufs, sem = refs[:k], refs[k:2 * k], refs[2 * k:3 * k], refs[3 * k]
-    loads = [pltpu.make_async_copy(ins[i], bufs[i], sem.at[0, i]) for i in range(k)]
-    stores = [pltpu.make_async_copy(bufs[i], outs[i], sem.at[1, i]) for i in range(k)]
-    for cp in loads:
+    k = len(refs) // 2
+    stores = [pltpu.make_async_copy(refs[i], refs[k + i], refs[2 * k].at[i]) for i in range(k)]
+    for cp in stores:
         cp.start()
-    for ld, st in zip(loads, stores):
-        ld.wait()
-        st.start()
     for cp in stores:
         cp.wait()
 
@@ -532,25 +521,26 @@
             vm((n_quad, n_hp, 2, 2, m_rows, LANES), F32), vm((group, rows, hdk), F32), vm((2, rows // 2, dm), F32),
             vm((fe // LANES, rows, LANES), F32), vm((fe // LANES, rows, LANES), BF16),
             vm((n_ch, 2, n_hp, rows // 2, LANES), F32), qblk, qblk, qblk, vm((n_ch, n_hp, 2, rows // 2, LANES), F32),
-        ] + [vm(o.shape, o.dtype) for o in outs] + [
-            dma((14,)), dma((n_hp,)), dma((2,)), dma((1,)), dma((4,)), dma((4,)), dma((2,)), dma((1,)), dma((3,)),
+            dma((14,)), dma((n_hp,)), dma((2,)), dma((1,)), dma((4,)), dma((4,)), dma((2,)), dma((1,)),
             dma((1,)), dma((n_quad,)), dma((1,)), dma((n_quad,)), dma((2,)), dma((n_quad, n_hp, 2)),
             dma((1,)), dma((n_ch,)), dma((1,)), dma((n_ch, n_hp)), dma((2,)), dma((n_ch, n_hp, 2)),
         ]
+        vmem_spec = pl.BlockSpec(memory_space=pltpu.VMEM)
         made = pl.pallas_call(
             functools.partial(layer_kernel, dims),
-            out_shape=outs,
+            out_shape=tuple(vm(o.shape, o.dtype) for o in outs),
             in_specs=[any_spec] * len(args),
-            out_specs=(any_spec,) * 3,
+            out_specs=(vmem_spec,) * 3,
             scratch_shapes=scratch,
-            compiler_params=pltpu.CompilerParams(collective_id=0, has_side_effects=True, vmem_limit_bytes=64 * 1024 * 1024),
+            compiler_params=pltpu.CompilerParams(collective_id=0, has_side_effects=True, vmem_limit_bytes=VMEM_BYTES),
         )(*args)
+        made = [pltpu.with_memory_space_constraint(m, pltpu.VMEM) for m in made]
         return pl.pallas_call(
             emit_kernel,
             out_shape=outs,
             in_specs=[any_spec] * 3,
             out_specs=(any_spec,) * 3,
-            scratch_shapes=[vm(o.shape, o.dtype) for o in outs] + [dma((2, 3))],
+            scratch_shapes=[dma((3,))],
         )(*made)
 
     replicated = P()

time: 43.5 us -> 41.8 us (0.961)
  Pallas kernels: 42.7 us -> 41.1 us
    pallas_call x1, Pallas kernels: 1.71 us -> 0.75 us  [layer_steps(): pl.pallas_call(emit_kernel, out_shape=outs, in_specs=[any_spec] * 3, out_...]
    pallas_call x1, Pallas kernels: 41 us -> 40.4 us  [layer_steps(): pl.pallas_call(functools.partial(layer_kernel, dims), out_shape=tuple((vm...]
where the time goes in v5:
time: 41.8 us
  Pallas kernels  41.1 us (98%)
  between operations  0.65 us (2%)
    pallas_call x1, Pallas kernels, layer_steps(): pl.pallas_call(functools.partial(layer_kernel, dims), out_shape=tuple((vm...  40.4 us

profile of v5, /device:TPU:113, one launch (start us, length us, event | category | flops | bytes accessed | tf_op | source)
XLA Modules:
  0.0 41.8 jit_solution(17427041570788808834)
XLA Ops:
  0.6 40.4 %shard_map.247 = (bf16[3,16,1536]{2,1,0:T(8,128)(2,1)S(1)}, bf16[16,3,8,64]{3,2,1,0:T(8,128)(2,1)S(1)}, bf16[16,3,8,64]{3,2,1,0:T(8,128)(2,1)S(1)}) custom-call(bf16[16,1536]{1,0:T(8,128)(2,1)} %x_first.1, bf16[2,16,1536]{2,1,0:T(8,128)(2,1)} %next_emb.1, bf16[16,512,512]{2,1,0:T(8,128)(2,1)} %bitcast.17, bf16[16,512,512]{2,1,0:T(8,128)(2,1)} %bitcast.18, ...), custom_call_target="tpu_custom_call" | custom-call | tf_op jit(solution)/shard_map/pallas_call | solution.py:529
  41.0 0.8 %shard_map.248 = (bf16[3,16,1536]{2,1,0:T(8,128)(2,1)}, bf16[16,3,8,64]{3,2,1,0:T(8,128)(2,1)}, bf16[16,3,8,64]{3,2,1,0:T(8,128)(2,1)}) custom-call(bf16[3,16,1536]{2,1,0:T(8,128)(2,1)S(1)} %get-tuple-element.6.refs_0_, bf16[16,3,8,64]{3,2,1,0:T(8,128)(2,1)S(1)} %get-tuple-element.7.refs_1_, bf16[16,3,8,64]{3,2,1,0:T(8,128)(2,1)S(1)} %get-tuple-element.8.refs_2_), custom_call_target="tpu_custom_call" | custom-call | tf_op jit(solution)/shard_map/pallas_call | solution.py:538

commit v6 on v5

--- a/solution.py
+++ b/solution.py
@@ -161,41 +161,43 @@
     tail_hp = 2 * core + lax.rem(chip, 2)
     tail_q = chip // 2 * 2
     brow = pl.ds(pl.multiple_of(tail_q * quad, SUBL), SUBL)
-    for q in range(n_quad):
-        tail_s[q, :m_rows] = jnp.zeros((m_rows, LANES), F32)
-        tail_s[q, m_rows:m_rows + SUBL] = jnp.full((SUBL, LANES), NEG_FILL, F32)
-        tail_s[q, m_rows + SUBL:] = jnp.zeros((SUBL, LANES), F32)
-        for hp in range(n_hp):
-            msg_s[q, hp, o_rows:] = jnp.zeros((quad, LANES), F32)
-    m_tail = jnp.full((SUBL, LANES), NEG_FILL, F32)
-    l_tail = jnp.zeros((SUBL, LANES), F32)
-    for gs in range(gs_n):
-        s = gs % steps
-        qt = q_s[tail_hp, gs, brow, :]
-        cols = []
-        for slot in range(s + 1):
-            prod = qt * kt_s[tail_hp, slot, brow, :]
-            lo = jnp.sum(jnp.where(low8, prod, 0.0), axis=1, keepdims=True)
-            hi = jnp.sum(jnp.where(low8, 0.0, prod), axis=1, keepdims=True)
-            cols.append(jnp.where(low8, lo, hi) * (hd ** -0.5))
-        mx = functools.reduce(jnp.maximum, cols)
-        ws = [jnp.exp(c - mx) for c in cols]
-        lsum = functools.reduce(jnp.add, ws)
-        acc = functools.reduce(jnp.add, [w.astype(BF16).astype(F32) * vt_s[tail_hp, slot, brow, :] for slot, w in enumerate(ws)])
+
+    def tail_slots():
+        for q in range(n_quad):
+            tail_s[q, :m_rows] = jnp.zeros((m_rows, LANES), F32)
+            tail_s[q, m_rows:m_rows + SUBL] = jnp.full((SUBL, LANES), NEG_FILL, F32)
+            tail_s[q, m_rows + SUBL:] = jnp.zeros((SUBL, LANES), F32)
+            for hp in range(n_hp):
+                msg_s[q, hp, o_rows:] = jnp.zeros((quad, LANES), F32)
+        m_tail = jnp.full((SUBL, LANES), NEG_FILL, F32)
+        l_tail = jnp.zeros((SUBL, LANES), F32)
+        for gs in range(gs_n):
+            s = gs % steps
+            qt = q_s[tail_hp, gs, brow, :]
+            cols = []
+            for slot in range(s + 1):
+                prod = qt * kt_s[tail_hp, slot, brow, :]
+                lo = jnp.sum(jnp.where(low8, prod, 0.0), axis=1, keepdims=True)
+                hi = jnp.sum(jnp.where(low8, 0.0, prod), axis=1, keepdims=True)
+                cols.append(jnp.where(low8, lo, hi) * (hd ** -0.5))
+            mx = functools.reduce(jnp.maximum, cols)
+            ws = [jnp.exp(c - mx) for c in cols]
+            lsum = functools.reduce(jnp.add, ws)
+            acc = functools.reduce(jnp.add, [w.astype(BF16).astype(F32) * vt_s[tail_hp, slot, brow, :] for slot, w in enumerate(ws)])
+            for i in range(2):
+                tail_s[tail_q + i, gs * quad:(gs + 1) * quad] = acc[i * quad:(i + 1) * quad]
+            for j in range(2):
+                sel = lane8 == gs * heads_kv + j
+                m_tail = jnp.where(sel, mx[:, j * hd:j * hd + 1], m_tail)
+                l_tail = jnp.where(sel, lsum[:, j * hd:j * hd + 1], l_tail)
+        m_tail = pltpu.roll(m_tail, 2 * tail_hp, 1)
+        l_tail = pltpu.roll(l_tail, 2 * tail_hp, 1)
         for i in range(2):
-            tail_s[tail_q + i, gs * quad:(gs + 1) * quad] = acc[i * quad:(i + 1) * quad]
-        for j in range(2):
-            sel = lane8 == gs * heads_kv + j
-            m_tail = jnp.where(sel, mx[:, j * hd:j * hd + 1], m_tail)
-            l_tail = jnp.where(sel, lsum[:, j * hd:j * hd + 1], l_tail)
-    m_tail = pltpu.roll(m_tail, 2 * tail_hp, 1)
-    l_tail = pltpu.roll(l_tail, 2 * tail_hp, 1)
-    for i in range(2):
-        for k in range(2):
-            rs = slice(m_rows + k * quad, m_rows + (k + 1) * quad)
-            tail_s[tail_q + i, rs] = m_tail[i * quad:(i + 1) * quad]
-            rs = slice(m_rows + SUBL + k * quad, m_rows + SUBL + (k + 1) * quad)
-            tail_s[tail_q + i, rs] = l_tail[i * quad:(i + 1) * quad]
+            for k in range(2):
+                rs = slice(m_rows + k * quad, m_rows + (k + 1) * quad)
+                tail_s[tail_q + i, rs] = m_tail[i * quad:(i + 1) * quad]
+                rs = slice(m_rows + SUBL + k * quad, m_rows + SUBL + (k + 1) * quad)
+                tail_s[tail_q + i, rs] = l_tail[i * quad:(i + 1) * quad]
 
     def to_row(col):
         return jnp.sum(jnp.where(ident, col, 0.0), axis=0, keepdims=True)
@@ -317,6 +319,8 @@
             ml_copy(i - 2).wait_recv()
         if i < n_quad:
             scores(i)
+        if i == 1:
+            tail_slots()
         if i:
             outputs(i - 1)
         if i > 1:

time: 41.8 us -> 41.9 us (level)
  no operation moved by 1% of the time
where the time goes in v6:
time: 41.9 us; the launch traced here: 41.8 us
  Pallas kernels  41.1 us (98%)
  between operations  0.65 us (2%)
    pallas_call x1, Pallas kernels, layer_steps(): pl.pallas_call(functools.partial(layer_kernel, dims), out_shape=tuple((vm...  40.4 us

profile of v6, /device:TPU:113, one launch (start us, length us, event | category | flops | bytes accessed | tf_op | source)
XLA Modules:
  0.0 41.8 jit_solution(13721545151785241539)
XLA Ops:
  0.6 40.4 %shard_map.247 = (bf16[3,16,1536]{2,1,0:T(8,128)(2,1)S(1)}, bf16[16,3,8,64]{3,2,1,0:T(8,128)(2,1)S(1)}, bf16[16,3,8,64]{3,2,1,0:T(8,128)(2,1)S(1)}) custom-call(bf16[16,1536]{1,0:T(8,128)(2,1)} %x_first.1, bf16[2,16,1536]{2,1,0:T(8,128)(2,1)} %next_emb.1, bf16[16,512,512]{2,1,0:T(8,128)(2,1)} %bitcast.17, bf16[16,512,512]{2,1,0:T(8,128)(2,1)} %bitcast.18, ...), custom_call_target="tpu_custom_call" | custom-call | tf_op jit(solution)/shard_map/pallas_call | solution.py:533
  41.0 0.8 %shard_map.248 = (bf16[3,16,1536]{2,1,0:T(8,128)(2,1)}, bf16[16,3,8,64]{3,2,1,0:T(8,128)(2,1)}, bf16[16,3,8,64]{3,2,1,0:T(8,128)(2,1)}) custom-call(bf16[3,16,1536]{2,1,0:T(8,128)(2,1)S(1)} %get-tuple-element.6.refs_0_, bf16[16,3,8,64]{3,2,1,0:T(8,128)(2,1)S(1)} %get-tuple-element.7.refs_1_, bf16[16,3,8,64]{3,2,1,0:T(8,128)(2,1)S(1)} %get-tuple-element.8.refs_2_), custom_call_target="tpu_custom_call" | custom-call | tf_op jit(solution)/shard_map/pallas_call | solution.py:542

commit v7 on v6

--- a/solution.py
+++ b/solution.py
@@ -87,6 +87,8 @@
 
     for cp in small_waits:
         cp.wait()
+    for cp in (k_copies[0], k_copies[1], v_copies[0]):
+        cp.start()
 
     g1, b1, bq, bo, g2, b2 = [vec_s[i].reshape(1, dm) for i in range(6)]
     x = x_s[...].reshape(rows, dm).astype(F32)
@@ -127,15 +129,15 @@
             c = c if c_hi else pltpu.roll(c, hd, 1)
             q_s[hp, g * steps:(g + 1) * steps] = jnp.where(low_head, a, c).reshape(steps, batch, LANES)
 
-    wq_copies[0].wait()
-    for cp in (k_copies[0], k_copies[1], v_copies[0], k_copies[2]):
+    for cp in wq_copies[:2]:
+        cp.wait()
+    for cp in (k_copies[2], v_copies[1]):
         cp.start()
-    wq_copies[1].wait()
     for hp in range(2):
         q_block(hp)
     for cp in wq_copies[2:] + wkv_copies:
         cp.wait()
-    for cp in (v_copies[1], k_copies[3], v_copies[2], v_copies[3]):
+    for cp in (k_copies[3], v_copies[2], v_copies[3]):
         cp.start()
     for hp in range(2, n_hp):
         q_block(hp)
@@ -375,21 +377,12 @@
         au = lax.dot_general(h2, wu_s[rs, :], NT, preferred_element_type=F32)
         return ag * (1.0 / (1.0 + jnp.exp(-ag))), au
 
-    peel = n_ec // 4
     for c in range(n_ec):
         gex_s[c] = jnp.where(low_head, gates[:, per * c:per * c + 1], gates[:, per * c + 1:per * c + 2])
-    for c in range(peel):
+    for c in range(n_ec):
         sg, au = act(c)
         u_s[c] = (gex_s[c] * sg * au).astype(BF16)
 
-    def expert(i, _):
-        for j in range(peel):
-            c = i * peel + j
-            sg, au = act(c)
-            u_s[c] = (gex_s[c] * sg * au).astype(BF16)
-        return 0
-
-    lax.fori_loop(1, n_ec // peel, expert, 0)
     cw = n_hp * LANES
     n_ch = dm // cw
     hr = rows // 2

time: 41.9 us -> 41.5 us (level)
  no operation moved by 1% of the time
where the time goes in v7:
time: 41.5 us
  Pallas kernels  40.8 us (98%)
  between operations  0.65 us (2%)
    pallas_call x1, Pallas kernels, layer_steps(): pl.pallas_call(functools.partial(layer_kernel, dims), out_shape=tuple((vm...  40.1 us

profile of v7, /device:TPU:113, one launch (start us, length us, event | category | flops | bytes accessed | tf_op | source)
XLA Modules:
  0.0 41.5 jit_solution(2386993521583069799)
XLA Ops:
  0.6 40.1 %shard_map.247 = (bf16[3,16,1536]{2,1,0:T(8,128)(2,1)S(1)}, bf16[16,3,8,64]{3,2,1,0:T(8,128)(2,1)S(1)}, bf16[16,3,8,64]{3,2,1,0:T(8,128)(2,1)S(1)}) custom-call(bf16[16,1536]{1,0:T(8,128)(2,1)} %x_first.1, bf16[2,16,1536]{2,1,0:T(8,128)(2,1)} %next_emb.1, bf16[16,512,512]{2,1,0:T(8,128)(2,1)} %bitcast.17, bf16[16,512,512]{2,1,0:T(8,128)(2,1)} %bitcast.18, ...), custom_call_target="tpu_custom_call" | custom-call | tf_op jit(solution)/shard_map/pallas_call | solution.py:526
  40.7 0.8 %shard_map.248 = (bf16[3,16,1536]{2,1,0:T(8,128)(2,1)}, bf16[16,3,8,64]{3,2,1,0:T(8,128)(2,1)}, bf16[16,3,8,64]{3,2,1,0:T(8,128)(2,1)}) custom-call(bf16[3,16,1536]{2,1,0:T(8,128)(2,1)S(1)} %get-tuple-element.6.refs_0_, bf16[16,3,8,64]{3,2,1,0:T(8,128)(2,1)S(1)} %get-tuple-element.7.refs_1_, bf16[16,3,8,64]{3,2,1,0:T(8,128)(2,1)S(1)} %get-tuple-element.8.refs_2_), custom_call_target="tpu_custom_call" | custom-call | tf_op jit(solution)/shard_map/pallas_call | solution.py:535

commit v8 on v7

--- a/solution.py
+++ b/solution.py
@@ -33,7 +33,7 @@
                  wq_s, wk_s, wv_s, wo_s, k_s, v_s, wg_s, wu_s, wd_s,
                  q_s, kt_s, vt_s, hs_s, p_s, msg_s, pair_s, ml_s, mlp_s, cf_s, tail_s, recv_s, of_s, xm_s, gex_s, u_s, pbuf_s, ppair_s, psum_s, rbuf_s, ybuf_s,
                  small_sem, wq_sem, wkv_sem, wo_sem, k_sem, v_sem, exp_sem, wd_sem,
-                 ml_send, ml_recv, pair_send, pair_recv, g_send, g_recv, d_send, d_recv, p_send, p_recv, y_send, y_recv):
+                 ml_send, ml_recv, pair_send, pair_recv, g_send, g_recv, d_send, d_recv, p_send, p_recv, y_send):
     n, steps, batch, heads_kv, hd, group, shard, n_exp, ff, dm = dims
     rows = steps * batch
     gs_n = group * steps
@@ -59,8 +59,15 @@
     qw = wq_s.shape[2]
     wq_copies = [pltpu.make_async_copy(wq_hbm.at[:, pl.ds(i * qw, qw)], wq_s.at[i], wq_sem.at[i]) for i in range(n_hp)]
     wkv_copies = [pltpu.make_async_copy(wk_hbm, wk_s, wkv_sem.at[0]), pltpu.make_async_copy(wv_hbm, wv_s, wkv_sem.at[1])]
-    for cp in small_copies + wq_copies + wkv_copies:
+    for cp in small_copies:
         cp.start()
+    cut = dm // 2
+    for j in range(2):
+        for i in range(n_hp):
+            pltpu.make_async_copy(wq_hbm.at[pl.ds(j * cut, cut), pl.ds(i * qw, qw)], wq_s.at[i, pl.ds(j * cut, cut)], wq_sem.at[i]).start()
+    for j in range(2):
+        for i, (src, dst) in enumerate(((wk_hbm, wk_s), (wv_hbm, wv_s))):
+            pltpu.make_async_copy(src.at[pl.ds(j * cut, cut)], dst.at[pl.ds(j * cut, cut)], wkv_sem.at[i]).start()
 
     barrier = pltpu.get_barrier_semaphore()
     for d in range(1, n):
@@ -73,6 +80,12 @@
         sl = pl.ds(i * quad, quad)
         return pltpu.make_async_copy(src.at[sl], dst.at[sl], sem.at[i])
 
+    def cache_start(src, dst, sem, i):
+        for b in range(i * quad, (i + 1) * quad):
+            pltpu.make_async_copy(src.at[b], dst.at[b], sem.at[i]).start()
+
+    k_start = functools.partial(cache_start, k_hbm, k_s, k_sem)
+    v_start = functools.partial(cache_start, v_hbm, v_s, v_sem)
     k_copies = [cache_copy(k_hbm, k_s, k_sem, i) for i in range(n_quad)]
     v_copies = [cache_copy(v_hbm, v_s, v_sem, i) for i in range(n_quad)]
     n_ec = wg_s.shape[0] // LANES
@@ -87,8 +100,9 @@
 
     for cp in small_waits:
         cp.wait()
-    for cp in (k_copies[0], k_copies[1], v_copies[0]):
-        cp.start()
+    k_start(0)
+    v_start(0)
+    k_start(1)
 
     g1, b1, bq, bo, g2, b2 = [vec_s[i].reshape(1, dm) for i in range(6)]
     x = x_s[...].reshape(rows, dm).astype(F32)
@@ -131,14 +145,15 @@
 
     for cp in wq_copies[:2]:
         cp.wait()
-    for cp in (k_copies[2], v_copies[1]):
-        cp.start()
+    k_start(2)
+    v_start(1)
     for hp in range(2):
         q_block(hp)
     for cp in wq_copies[2:] + wkv_copies:
         cp.wait()
-    for cp in (k_copies[3], v_copies[2], v_copies[3]):
-        cp.start()
+    k_start(3)
+    v_start(2)
+    v_start(3)
     for hp in range(2, n_hp):
         q_block(hp)
     t = jnp.dot(h, wk_s[...], preferred_element_type=F32) + bk_s[...].reshape(1, hdk)
@@ -306,35 +321,37 @@
                             r = gs % steps * batch + q * quad
                             of_s[gs // steps, r:r + quad, hp * LANES:(hp + 1) * LANES] = o[i * quad:(i + 1) * quad]
 
-    for i in range(n_quad + 1):
-        if i < n_quad:
-            k_copies[i].wait()
-        if i:
-            v_copies[i - 1].wait()
-        if i == n_quad - 1:
+    stages = [(0, None, None), (None, 0, None), (1, None, 0)]
+    stages += [(i + 1 if i + 1 < n_quad else None, i, i - 1 if i > 1 else None) for i in range(1, n_quad)]
+    for sc, out, mg in stages:
+        if sc is not None:
+            k_copies[sc].wait()
+        if out is not None:
+            v_copies[out].wait()
+        if sc == n_quad - 1:
             for g in range(group):
                 pltpu.make_async_copy(wo_hbm.at[:, :, g], wo_s.at[:, g], wo_sem.at[0]).start()
             weight_start(wg_hbm, wg_s, exp_sem.at[0])
             weight_start(wu_hbm, wu_s, exp_sem.at[1])
             weight_start(wd_hbm, wd_s, wd_sem.at[0])
-        if i > 1:
-            ml_copy(i - 2).wait_recv()
-        if i < n_quad:
-            scores(i)
-        if i == 1:
+        if mg is not None:
+            ml_copy(mg).wait_recv()
+        if sc is not None:
+            scores(sc)
+        if out == 0:
             tail_slots()
-        if i:
-            outputs(i - 1)
-        if i > 1:
-            pair_factors(i - 2)
-        if i == 0:
+        if out is not None:
+            outputs(out)
+        if mg is not None:
+            pair_factors(mg)
+        if sc == 0:
             pl.semaphore_wait(barrier, n - 1)
-        if i < n_quad:
-            ml_copy(i).start()
-        if i:
-            pair_copy(i - 1).start()
-        if i > 1:
-            pair_merge(i - 2)
+        if sc is not None:
+            ml_copy(sc).start()
+        if out is not None:
+            pair_copy(out).start()
+        if mg is not None:
+            pair_merge(mg)
     ml_copy(n_quad - 1).wait_recv()
     pair_factors(n_quad - 1)
     pair_merge(n_quad - 1)
@@ -420,7 +437,7 @@
 
     def y_arrived(k, cx, c):
         blk = ybuf_s.at[k, cx, c]
-        remote(blk, blk, y_send.at[0], y_recv.at[k, cx, c], me).wait_recv()
+        remote(blk, blk, y_send.at[0], g_recv.at[k, cx, c], me).wait_recv()
         return blk
 
     for k in range(n_ch):
@@ -432,13 +449,13 @@
         ybuf_s[k, chip, core] = y.astype(BF16).astype(F32)
         blk = ybuf_s.at[k, chip, core]
         for dx in (2, 1, 3):
-            remote(blk, blk, y_send.at[0], y_recv.at[k, chip, core], lax.rem(chip + dx, n_hp) * 2 + core).start()
-        remote(blk, blk, y_send.at[1], y_recv.at[k, chip, core], partner).start()
+            remote(blk, blk, y_send.at[0], g_recv.at[k, chip, core], lax.rem(chip + dx, n_hp) * 2 + core).start()
+        remote(blk, blk, y_send.at[1], g_recv.at[k, chip, core], partner).start()
     for k in range(n_ch):
         for dx in (1, 3, 2):
             cx = lax.rem(chip + dx, n_hp)
             blk = y_arrived(k, cx, core)
-            remote(blk, blk, y_send.at[1], y_recv.at[k, cx, core], partner).start()
+            remote(blk, blk, y_send.at[1], g_recv.at[k, cx, core], partner).start()
     for k in range(n_ch):
         for dx in (0, 1, 3, 2):
             y_arrived(k, lax.rem(chip + dx, n_hp), other)
@@ -520,7 +537,7 @@
             vm((n_ch, 2, n_hp, rows // 2, LANES), F32), qblk, qblk, qblk, vm((n_ch, n_hp, 2, rows // 2, LANES), F32),
             dma((14,)), dma((n_hp,)), dma((2,)), dma((1,)), dma((4,)), dma((4,)), dma((2,)), dma((1,)),
             dma((1,)), dma((n_quad,)), dma((1,)), dma((n_quad,)), dma((2,)), dma((n_quad, n_hp, 2)),
-            dma((1,)), dma((n_ch,)), dma((1,)), dma((n_ch, n_hp)), dma((2,)), dma((n_ch, n_hp, 2)),
+            dma((1,)), dma((n_ch,)), dma((1,)), dma((n_ch, n_hp)), dma((2,)),
         ]
         vmem_spec = pl.BlockSpec(memory_space=pltpu.VMEM)
         made = pl.pallas_call(

time: 41.5 us -> 41.6 us (level)
  no operation moved by 1% of the time
where the time goes in v8:
time: 41.6 us; the launch traced here: 41.5 us
  Pallas kernels  40.9 us (98%)
  between operations  0.65 us (2%)
    pallas_call x1, Pallas kernels, layer_steps(): pl.pallas_call(functools.partial(layer_kernel, dims), out_shape=tuple((vm...  40.1 us

profile of v8, /device:TPU:113, one launch (start us, length us, event | category | flops | bytes accessed | tf_op | source)
XLA Modules:
  0.0 41.5 jit_solution(5073691626074017112)
XLA Ops:
  0.6 40.1 %shard_map.247 = (bf16[3,16,1536]{2,1,0:T(8,128)(2,1)S(1)}, bf16[16,3,8,64]{3,2,1,0:T(8,128)(2,1)S(1)}, bf16[16,3,8,64]{3,2,1,0:T(8,128)(2,1)S(1)}) custom-call(bf16[16,1536]{1,0:T(8,128)(2,1)} %x_first.1, bf16[2,16,1536]{2,1,0:T(8,128)(2,1)} %next_emb.1, bf16[16,512,512]{2,1,0:T(8,128)(2,1)} %bitcast.17, bf16[16,512,512]{2,1,0:T(8,128)(2,1)} %bitcast.18, ...), custom_call_target="tpu_custom_call" | custom-call | tf_op jit(solution)/shard_map/pallas_call | solution.py:543
  40.8 0.8 %shard_map.248 = (bf16[3,16,1536]{2,1,0:T(8,128)(2,1)}, bf16[16,3,8,64]{3,2,1,0:T(8,128)(2,1)}, bf16[16,3,8,64]{3,2,1,0:T(8,128)(2,1)}) custom-call(bf16[3,16,1536]{2,1,0:T(8,128)(2,1)S(1)} %get-tuple-element.6.refs_0_, bf16[16,3,8,64]{3,2,1,0:T(8,128)(2,1)S(1)} %get-tuple-element.7.refs_1_, bf16[16,3,8,64]{3,2,1,0:T(8,128)(2,1)S(1)} %get-tuple-element.8.refs_2_), custom_call_target="tpu_custom_call" | custom-call | tf_op jit(solution)/shard_map/pallas_call | solution.py:552

commit v9 on v7

--- a/solution.py
+++ b/solution.py
@@ -33,7 +33,7 @@
                  wq_s, wk_s, wv_s, wo_s, k_s, v_s, wg_s, wu_s, wd_s,
                  q_s, kt_s, vt_s, hs_s, p_s, msg_s, pair_s, ml_s, mlp_s, cf_s, tail_s, recv_s, of_s, xm_s, gex_s, u_s, pbuf_s, ppair_s, psum_s, rbuf_s, ybuf_s,
                  small_sem, wq_sem, wkv_sem, wo_sem, k_sem, v_sem, exp_sem, wd_sem,
-                 ml_send, ml_recv, pair_send, pair_recv, g_send, g_recv, d_send, d_recv, p_send, p_recv, y_send, y_recv):
+                 ml_send, ml_recv, pair_send, pair_recv, g_send, g_recv, d_send, d_recv, p_send, p_recv, y_send):
     n, steps, batch, heads_kv, hd, group, shard, n_exp, ff, dm = dims
     rows = steps * batch
     gs_n = group * steps
@@ -420,7 +420,7 @@
 
     def y_arrived(k, cx, c):
         blk = ybuf_s.at[k, cx, c]
-        remote(blk, blk, y_send.at[0], y_recv.at[k, cx, c], me).wait_recv()
+        remote(blk, blk, y_send.at[0], g_recv.at[k, cx, c], me).wait_recv()
         return blk
 
     for k in range(n_ch):
@@ -432,13 +432,13 @@
         ybuf_s[k, chip, core] = y.astype(BF16).astype(F32)
         blk = ybuf_s.at[k, chip, core]
         for dx in (2, 1, 3):
-            remote(blk, blk, y_send.at[0], y_recv.at[k, chip, core], lax.rem(chip + dx, n_hp) * 2 + core).start()
-        remote(blk, blk, y_send.at[1], y_recv.at[k, chip, core], partner).start()
+            remote(blk, blk, y_send.at[0], g_recv.at[k, chip, core], lax.rem(chip + dx, n_hp) * 2 + core).start()
+        remote(blk, blk, y_send.at[1], g_recv.at[k, chip, core], partner).start()
     for k in range(n_ch):
         for dx in (1, 3, 2):
             cx = lax.rem(chip + dx, n_hp)
             blk = y_arrived(k, cx, core)
-            remote(blk, blk, y_send.at[1], y_recv.at[k, cx, core], partner).start()
+            remote(blk, blk, y_send.at[1], g_recv.at[k, cx, core], partner).start()
     for k in range(n_ch):
         for dx in (0, 1, 3, 2):
             y_arrived(k, lax.rem(chip + dx, n_hp), other)
@@ -520,7 +520,7 @@
             vm((n_ch, 2, n_hp, rows // 2, LANES), F32), qblk, qblk, qblk, vm((n_ch, n_hp, 2, rows // 2, LANES), F32),
             dma((14,)), dma((n_hp,)), dma((2,)), dma((1,)), dma((4,)), dma((4,)), dma((2,)), dma((1,)),
             dma((1,)), dma((n_quad,)), dma((1,)), dma((n_quad,)), dma((2,)), dma((n_quad, n_hp, 2)),
-            dma((1,)), dma((n_ch,)), dma((1,)), dma((n_ch, n_hp)), dma((2,)), dma((n_ch, n_hp, 2)),
+            dma((1,)), dma((n_ch,)), dma((1,)), dma((n_ch, n_hp)), dma((2,)),
         ]
         vmem_spec = pl.BlockSpec(memory_space=pltpu.VMEM)
         made = pl.pallas_call(

time: 41.5 us -> 41.3 us (level)
  no operation moved by 1% of the time
where the time goes in v9:
time: 41.3 us; the launch traced here: 41.2 us
  Pallas kernels  40.6 us (98%)
  between operations  0.65 us (2%)
    pallas_call x1, Pallas kernels, layer_steps(): pl.pallas_call(functools.partial(layer_kernel, dims), out_shape=tuple((vm...  39.8 us

profile of v9, /device:TPU:113, one launch (start us, length us, event | category | flops | bytes accessed | tf_op | source)
XLA Modules:
  0.0 41.2 jit_solution(13870391458842993000)
XLA Ops:
  0.6 39.8 %shard_map.247 = (bf16[3,16,1536]{2,1,0:T(8,128)(2,1)S(1)}, bf16[16,3,8,64]{3,2,1,0:T(8,128)(2,1)S(1)}, bf16[16,3,8,64]{3,2,1,0:T(8,128)(2,1)S(1)}) custom-call(bf16[16,1536]{1,0:T(8,128)(2,1)} %x_first.1, bf16[2,16,1536]{2,1,0:T(8,128)(2,1)} %next_emb.1, bf16[16,512,512]{2,1,0:T(8,128)(2,1)} %bitcast.17, bf16[16,512,512]{2,1,0:T(8,128)(2,1)} %bitcast.18, ...), custom_call_target="tpu_custom_call" | custom-call | tf_op jit(solution)/shard_map/pallas_call | solution.py:526
  40.5 0.8 %shard_map.248 = (bf16[3,16,1536]{2,1,0:T(8,128)(2,1)}, bf16[16,3,8,64]{3,2,1,0:T(8,128)(2,1)}, bf16[16,3,8,64]{3,2,1,0:T(8,128)(2,1)}) custom-call(bf16[3,16,1536]{2,1,0:T(8,128)(2,1)S(1)} %get-tuple-element.6.refs_0_, bf16[16,3,8,64]{3,2,1,0:T(8,128)(2,1)S(1)} %get-tuple-element.7.refs_1_, bf16[16,3,8,64]{3,2,1,0:T(8,128)(2,1)S(1)} %get-tuple-element.8.refs_2_), custom_call_target="tpu_custom_call" | custom-call | tf_op jit(solution)/shard_map/pallas_call | solution.py:535
